TPU v7x, 256 devices: a whole 4x4x8 slice. The times are simulated.
256 devices in a mesh: sub: 32 (over z, x_lo, core), row: 8 (over y, x_hi).
Axes of the slice: x: 4 (x_hi: 2, x_lo: 2; x = x_hi * 2 + x_lo), y: 4, z: 8, core: 2. Of those that a mesh axis runs over, the one named last changes fastest.
Arguments:
- factor_blocks: float32 [32, 32, 3, 256, 256], P('sub', 'row'), may hold values from -0.25 to 0.25
- block_inverses: float32 [32, 32, 256, 256], P('sub', 'row'), as said below
- band_offsets: int32 [32, 32, 3], P('sub', 'row'), may hold values from 1 to 4, as said below
- coupling: float32 [32, 8192, 512], P('sub', 'row'), may hold values from -0.0625 to 0.0625
- interface_block: float32 [32, 4, 128, 512], P('sub', None, 'row'), may hold values from -6 to 6
- tile_ids: int32 [32, 4], replicated, may hold values from 0 to 255, as said below
Outputs:
- schur_tiles: float32 [32, 4, 128, 512], P('sub', None, 'row')
Inputs may be any that keep to these rules, and one draw needn't show every extreme that they name: `band_offsets`: each entry is one of the numbers 1 .. 4, the 3 entries of a block row are distinct and rising. `tile_ids`: A subdomain's 4 numbers are distinct; a number appears in at most two subdomains, and then in neighbouring ones (s and s + 1); every subdomain but the last shares one or two numbers with the next. `block_inverses`: each block is lower triangular with a diagonal between 0.5 and 1.
All inputs are finite; a program needn't handle non-finite values.
Results may differ from a plain program's by a relative error of at most 0.0003.
Values sent between devices are 32-bit elements; how exact they have to be, the bound alone decides.
A program may use at most 64 MiB of HBM per device.

v0:
```python
import jax
import jax.numpy as jnp
from jax import lax
from jax.sharding import PartitionSpec as P


def from_behind(value, axis, steps):
    count = lax.axis_size(axis)
    first, last = (max(0, -steps), min(count, count - steps))
    return lax.ppermute(value, axis, [(source, source + steps) for source in range(first, last)])


def in_blocks(value, dim, size):
    lengths = value.shape
    parts = value.reshape(*lengths[:dim], size, lengths[dim] // size, *lengths[dim + 1 :])
    return jnp.moveaxis(parts, dim, 0)


def sent_and_summed(value, axis, dim):
    size = lax.axis_size(axis)
    parts = lax.all_to_all(in_blocks(value, dim, size), axis, 0, 0, tiled=True)
    return jnp.sum(parts, axis=0)


def padded(block, sides, width):
    for axis, dim in sides:
        count = lax.axis_size(axis)
        forward = [(i, i + 1) for i in range(count - 1)]
        backward = [(target, source) for source, target in forward]
        low = lax.ppermute(
            lax.slice_in_dim(block, block.shape[dim] - width, None, axis=dim), axis, forward
        )
        high = lax.ppermute(lax.slice_in_dim(block, 0, width, axis=dim), axis, backward)
        block = jnp.concatenate([low, block, high], axis=dim)
    return block


def shards(factor_blocks, block_inverses, band_offsets, coupling, interface_block, tile_ids):
    blocks = factor_blocks[0]
    inverses = block_inverses[0]
    offsets = band_offsets[0]
    brows = blocks.shape[0]
    kband = blocks.shape[1]
    block_size = blocks.shape[2]
    panel_cols = coupling.shape[2]
    right_side = coupling[0].reshape(brows, block_size, panel_cols)
    row_index = lax.axis_index("row")
    row_count = lax.axis_size("row")

    def solve(incoming, right):
        extended = jnp.concatenate([incoming, jnp.zeros_like(right)], 0)

        def substitute(row_block, extended):
            running = lax.dynamic_index_in_dim(right, row_block, 0, keepdims=False)
            factor_row = lax.dynamic_index_in_dim(blocks, row_block, 0, keepdims=False)
            offset_row = lax.dynamic_index_in_dim(offsets, row_block, 0, keepdims=False)
            for band in range(kband):
                source_index = brows + row_block - offset_row[band]
                source = lax.dynamic_index_in_dim(extended, source_index, 0, keepdims=False)
                running = running - jnp.dot(
                    factor_row[band], source, precision=lax.Precision.HIGHEST
                )
            inverse = lax.dynamic_index_in_dim(inverses, row_block, 0, keepdims=False)
            solved_row = jnp.dot(inverse, running, precision=lax.Precision.HIGHEST)
            return lax.dynamic_update_index_in_dim(
                extended, solved_row, (brows + row_block).astype(jnp.int32), 0
            )

        extended = lax.fori_loop(jnp.int32(0), jnp.int32(brows), substitute, extended)
        return extended[brows:]

    empty = jnp.zeros_like(right_side)
    column_parts = 4
    block_cols = panel_cols // column_parts

    def advance(section_index, carried):
        solved, outgoing = carried
        incoming = from_behind(outgoing, "row", 1)
        column = section_index - row_index
        active = (column >= 0) & (column < column_parts)
        column_start = jnp.clip(column, 0, column_parts - 1) * block_cols

        def compute():
            solved_piece = solve(
                incoming, lax.dynamic_slice_in_dim(right_side, column_start, block_cols, 2)
            )
            return (
                lax.dynamic_update_slice_in_dim(solved, solved_piece, column_start, 2),
                solved_piece,
            )

        return lax.cond(active, compute, lambda: (solved, jnp.zeros_like(outgoing)))

    start_piece = jnp.zeros((brows, block_size, block_cols), jnp.float32)
    solved, outgoing = lax.fori_loop(0, row_count + column_parts - 1, advance, (empty, start_piece))
    flattened = solved.reshape(brows * block_size, panel_cols)
    partial_value = lax.dot_general(
        flattened,
        flattened,
        (((0,), (0,)), ((), ())),
        precision=lax.Precision.HIGHEST,
        preferred_element_type=jnp.float32,
    )
    tile_count = interface_block.shape[1]
    tile_size = panel_cols // tile_count
    row_share = interface_block.shape[2]
    partial_value = partial_value.reshape(tile_count, tile_size, panel_cols)
    sub_index = lax.axis_index("sub")
    sub_total = tile_ids.shape[0]
    neighbour_ids = [
        lax.dynamic_index_in_dim(
            tile_ids, jnp.clip(sub_index + delta, 0, sub_total - 1), 0, keepdims=False
        )
        for delta in (-1, 0, 1)
    ]
    own_ids = neighbour_ids[1]
    match = jnp.stack(
        [(own_ids[:, None] == other[None, :]).astype(jnp.float32) for other in neighbour_ids]
    )
    gram_rows = sent_and_summed(partial_value, "row", 1)
    nearby = padded(gram_rows[None], (("sub", 0),), 1)
    nearby = nearby.reshape(3, tile_count, row_share, tile_count, tile_size)
    contribution = jnp.einsum(
        "tik,tjl,tkalb->iajb", match, match, nearby, precision=lax.Precision.HIGHEST
    )
    assembled = interface_block[0] - contribution.reshape(tile_count, row_share, panel_cols)
    return assembled[None]


def solution(mesh):
    return jax.shard_map(
        shards,
        mesh=mesh,
        in_specs=(
            P("sub", "row", None, None, None),
            P("sub", "row", None, None),
            P("sub", "row", None),
            P("sub", "row", None),
            P("sub", None, "row", None),
            P(),
        ),
        out_specs=P("sub", None, "row", None),
        check_vma=False,
    )
```

profile of v0, /device:TPU:107, one launch (start us, length us, event | category | flops | bytes accessed | tf_op | source)
XLA Modules:
  0.0 559.8 jit_solution(8853029029347489469)
XLA Ops:
  0.8 1.6 broadcast_in_dim.20
  3.2 413.8 %while.32 = (s32[]{:T(128)}, f32[4,256,512]{2,1,0:T(8,128)}, f32[4,256,128]{2,1,0:T(8,128)}, s32[]{:T(128)}, f32[4,256,512]{2,1,0:T(8,128)}, /*index=5*/f32[4,25...) while((s32[]{:T(128)}, f32[4,256,512]{2,1,0:T(8,128)}, ...), condition=%wide.region_5.6_spmd, body=%wide.region_0.5_spmd.sunk | while | flops 402751488 | bytes 8784238 | solution.py:95
  3.2 3.7 collective-permute-start
  7.0 13.5 %collective-permute-done = f32[4,256,128]{2,1,0:T(8,128)S(1)} collective-permute-done((f32[4,256,128]{2,1,0:T(8,128)}, f32[4,256,128]{2,1,0:T(8,128)S(1)}, u32[]{:S(2)}, u32[]{:S(2)}) %collective-permute-start) | collective-permute-done | bytes 524320 | tf_op jit(solution)/shard_map/while/body/eval_jaxpr/ppermute | solution.py:10
  21.3 2.8 collective-permute-start
  24.2 13.6 %collective-permute-done = f32[4,256,128]{2,1,0:T(8,128)S(1)} collective-permute-done((f32[4,256,128]{2,1,0:T(8,128)}, f32[4,256,128]{2,1,0:T(8,128)S(1)}, u32[]{:S(2)}, u32[]{:S(2)}) %collective-permute-start) | collective-permute-done | bytes 524320 | tf_op jit(solution)/shard_map/while/body/eval_jaxpr/ppermute | solution.py:10
  38.6 1.9 collective-permute-start
  40.6 72.2 %collective-permute-done = f32[4,256,128]{2,1,0:T(8,128)S(1)} collective-permute-done((f32[4,256,128]{2,1,0:T(8,128)}, f32[4,256,128]{2,1,0:T(8,128)S(1)}, u32[]{:S(2)}, u32[]{:S(2)}) %collective-permute-start) | collective-permute-done | bytes 524320 | tf_op jit(solution)/shard_map/while/body/eval_jaxpr/ppermute | solution.py:10
  112.8 33.8 %conditional.2 = ((f32[4,256,512]{2,1,0:T(8,128)}, f32[4,256,128]{2,1,0:T(8,128)})) conditional(s32[]{:T(128)} %convert_element_type.32, f32[4,256,512]{2,1,0:T(8,128)} %get-tuple-element.462, (f32[4,256,128]{2,1,0:T(8,128)S(1)}, s32[]{:T(128)}, f32[4,256,512]{2,1,0:T(8,128)}, f32[4,256,256]{2,1,0:T(8,128)}, f32[4,3,256,256]{3,2,1,0:T(8,128)}, ...), branch_computations={%region_1.1_spmd, %region_2.4_spmd} | conditional | flops 402751488 | bytes 6686835 | solution.py:92
  113.9 31.5 %while.31 = (s32[]{:T(128)}, f32[8,256,128]{2,1,0:T(8,128)S(1)}, f32[4,256,256]{2,1,0:T(8,128)}, f32[4,256,128]{2,1,0:T(8,128)S(1)}, f32[4,3,256,256]{3,2,1,0:T(...) while((s32[]{:T(128)}, f32[8,256,128]{2,1,0:T(8,128)S(1)}, ...), condition=%wide.region_4.3_spmd, body=%wide.region_3.2_spmd.sunk | while | flops 402751488 | bytes 2492329 | solution.py:69
  117.2 1.3 convolution_subtract_fusion.7
  119.1 1.3 convolution_subtract_fusion.8
  123.1 1.3 convolution_subtract_fusion.6
  125.0 1.3 convolution_subtract_fusion.7
  131.0 1.3 convolution_subtract_fusion.6
  132.9 1.3 convolution_subtract_fusion.7
  134.9 1.3 convolution_subtract_fusion.8
  138.8 1.3 convolution_subtract_fusion.6
  140.8 1.3 convolution_subtract_fusion.7
  142.8 1.3 convolution_subtract_fusion.8
  146.6 1.9 collective-permute-start
  148.5 13.3 %collective-permute-done = f32[4,256,128]{2,1,0:T(8,128)S(1)} collective-permute-done((f32[4,256,128]{2,1,0:T(8,128)}, f32[4,256,128]{2,1,0:T(8,128)S(1)}, u32[]{:S(2)}, u32[]{:S(2)}) %collective-permute-start) | collective-permute-done | bytes 524320 | tf_op jit(solution)/shard_map/while/body/eval_jaxpr/ppermute | solution.py:10
  161.8 33.8 %conditional.2 = ((f32[4,256,512]{2,1,0:T(8,128)}, f32[4,256,128]{2,1,0:T(8,128)})) conditional(s32[]{:T(128)} %convert_element_type.32, f32[4,256,512]{2,1,0:T(8,128)} %get-tuple-element.462, (f32[4,256,128]{2,1,0:T(8,128)S(1)}, s32[]{:T(128)}, f32[4,256,512]{2,1,0:T(8,128)}, f32[4,256,256]{2,1,0:T(8,128)}, f32[4,3,256,256]{3,2,1,0:T(8,128)}, ...), branch_computations={%region_1.1_spmd, %region_2.4_spmd} | conditional | flops 402751488 | bytes 6686835 | solution.py:92
  163.0 31.5 %while.31 = (s32[]{:T(128)}, f32[8,256,128]{2,1,0:T(8,128)S(1)}, f32[4,256,256]{2,1,0:T(8,128)}, f32[4,256,128]{2,1,0:T(8,128)S(1)}, f32[4,3,256,256]{3,2,1,0:T(...) while((s32[]{:T(128)}, f32[8,256,128]{2,1,0:T(8,128)S(1)}, ...), condition=%wide.region_4.3_spmd, body=%wide.region_3.2_spmd.sunk | while | flops 402751488 | bytes 2492329 | solution.py:69
  164.2 1.3 convolution_subtract_fusion.6
  166.2 1.3 convolution_subtract_fusion.7
  168.2 1.3 convolution_subtract_fusion.8
  174.1 1.3 convolution_subtract_fusion.7
  176.1 1.3 convolution_subtract_fusion.8
  182.0 1.3 convolution_subtract_fusion.7
  183.9 1.3 convolution_subtract_fusion.8
  189.8 1.3 convolution_subtract_fusion.7
  195.6 1.9 collective-permute-start
  197.6 12.4 %collective-permute-done = f32[4,256,128]{2,1,0:T(8,128)S(1)} collective-permute-done((f32[4,256,128]{2,1,0:T(8,128)}, f32[4,256,128]{2,1,0:T(8,128)S(1)}, u32[]{:S(2)}, u32[]{:S(2)}) %collective-permute-start) | collective-permute-done | bytes 524320 | tf_op jit(solution)/shard_map/while/body/eval_jaxpr/ppermute | solution.py:10
  210.0 33.8 %conditional.2 = ((f32[4,256,512]{2,1,0:T(8,128)}, f32[4,256,128]{2,1,0:T(8,128)})) conditional(s32[]{:T(128)} %convert_element_type.32, f32[4,256,512]{2,1,0:T(8,128)} %get-tuple-element.462, (f32[4,256,128]{2,1,0:T(8,128)S(1)}, s32[]{:T(128)}, f32[4,256,512]{2,1,0:T(8,128)}, f32[4,256,256]{2,1,0:T(8,128)}, f32[4,3,256,256]{3,2,1,0:T(8,128)}, ...), branch_computations={%region_1.1_spmd, %region_2.4_spmd} | conditional | flops 402751488 | bytes 6686835 | solution.py:92
  211.2 31.5 %while.31 = (s32[]{:T(128)}, f32[8,256,128]{2,1,0:T(8,128)S(1)}, f32[4,256,256]{2,1,0:T(8,128)}, f32[4,256,128]{2,1,0:T(8,128)S(1)}, f32[4,3,256,256]{3,2,1,0:T(...) while((s32[]{:T(128)}, f32[8,256,128]{2,1,0:T(8,128)S(1)}, ...), condition=%wide.region_4.3_spmd, body=%wide.region_3.2_spmd.sunk | while | flops 402751488 | bytes 2492329 | solution.py:69
  214.4 1.3 convolution_subtract_fusion.7
  220.3 1.3 convolution_subtract_fusion.6
  222.3 1.3 convolution_subtract_fusion.7
  224.3 1.3 convolution_subtract_fusion.8
  228.2 1.3 convolution_subtract_fusion.6
  230.2 1.3 convolution_subtract_fusion.7
  236.1 1.3 convolution_subtract_fusion.6
  238.0 1.3 convolution_subtract_fusion.7
  243.8 1.9 collective-permute-start
  245.7 11.6 %collective-permute-done = f32[4,256,128]{2,1,0:T(8,128)S(1)} collective-permute-done((f32[4,256,128]{2,1,0:T(8,128)}, f32[4,256,128]{2,1,0:T(8,128)S(1)}, u32[]{:S(2)}, u32[]{:S(2)}) %collective-permute-start) | collective-permute-done | bytes 524320 | tf_op jit(solution)/shard_map/while/body/eval_jaxpr/ppermute | solution.py:10
  257.3 33.7 %conditional.2 = ((f32[4,256,512]{2,1,0:T(8,128)}, f32[4,256,128]{2,1,0:T(8,128)})) conditional(s32[]{:T(128)} %convert_element_type.32, f32[4,256,512]{2,1,0:T(8,128)} %get-tuple-element.462, (f32[4,256,128]{2,1,0:T(8,128)S(1)}, s32[]{:T(128)}, f32[4,256,512]{2,1,0:T(8,128)}, f32[4,256,256]{2,1,0:T(8,128)}, f32[4,3,256,256]{3,2,1,0:T(8,128)}, ...), branch_computations={%region_1.1_spmd, %region_2.4_spmd} | conditional | flops 402751488 | bytes 6686835 | solution.py:92
  258.5 31.5 %while.31 = (s32[]{:T(128)}, f32[8,256,128]{2,1,0:T(8,128)S(1)}, f32[4,256,256]{2,1,0:T(8,128)}, f32[4,256,128]{2,1,0:T(8,128)S(1)}, f32[4,3,256,256]{3,2,1,0:T(...) while((s32[]{:T(128)}, f32[8,256,128]{2,1,0:T(8,128)S(1)}, ...), condition=%wide.region_4.3_spmd, body=%wide.region_3.2_spmd.sunk | while | flops 402751488 | bytes 2492329 | solution.py:69
  291.1 1.9 collective-permute-start
  293.0 10.6 %collective-permute-done = f32[4,256,128]{2,1,0:T(8,128)S(1)} collective-permute-done((f32[4,256,128]{2,1,0:T(8,128)}, f32[4,256,128]{2,1,0:T(8,128)S(1)}, u32[]{:S(2)}, u32[]{:S(2)}) %collective-permute-start) | collective-permute-done | bytes 524320 | tf_op jit(solution)/shard_map/while/body/eval_jaxpr/ppermute | solution.py:10
  304.4 34.4 %collective-permute-start = (f32[4,256,128]{2,1,0:T(8,128)}, f32[4,256,128]{2,1,0:T(8,128)S(1)}, u32[]{:S(2)}, u32[]{:S(2)}) collective-permute-start(f32[4,256,128]{2,1,0:T(8,128)} %get-tuple-element.463), channel_id=1, source_target_pairs={{0,1},{1,2},{2,3},{3,4},{4,5},{5,6},{6,7},{8,9},{9,10},{10,11},{11... | collective-permute-start | bytes 1572872 | tf_op jit(solution)/shard_map/while/body/eval_jaxpr/ppermute | solution.py:10
  338.8 6.4 %collective-permute-done = f32[4,256,128]{2,1,0:T(8,128)S(1)} collective-permute-done((f32[4,256,128]{2,1,0:T(8,128)}, f32[4,256,128]{2,1,0:T(8,128)S(1)}, u32[]{:S(2)}, u32[]{:S(2)}) %collective-permute-start) | collective-permute-done | bytes 524320 | tf_op jit(solution)/shard_map/while/body/eval_jaxpr/ppermute | solution.py:10
  346.1 5.2 collective-permute-start
  351.3 7.3 %collective-permute-done = f32[4,256,128]{2,1,0:T(8,128)S(1)} collective-permute-done((f32[4,256,128]{2,1,0:T(8,128)}, f32[4,256,128]{2,1,0:T(8,128)S(1)}, u32[]{:S(2)}, u32[]{:S(2)}) %collective-permute-start) | collective-permute-done | bytes 524320 | tf_op jit(solution)/shard_map/while/body/eval_jaxpr/ppermute | solution.py:10
  359.4 36.5 %collective-permute-start = (f32[4,256,128]{2,1,0:T(8,128)}, f32[4,256,128]{2,1,0:T(8,128)S(1)}, u32[]{:S(2)}, u32[]{:S(2)}) collective-permute-start(f32[4,256,128]{2,1,0:T(8,128)} %get-tuple-element.463), channel_id=1, source_target_pairs={{0,1},{1,2},{2,3},{3,4},{4,5},{5,6},{6,7},{8,9},{9,10},{10,11},{11... | collective-permute-start | bytes 1572872 | tf_op jit(solution)/shard_map/while/body/eval_jaxpr/ppermute | solution.py:10
  396.0 6.4 %collective-permute-done = f32[4,256,128]{2,1,0:T(8,128)S(1)} collective-permute-done((f32[4,256,128]{2,1,0:T(8,128)}, f32[4,256,128]{2,1,0:T(8,128)S(1)}, u32[]{:S(2)}, u32[]{:S(2)}) %collective-permute-start) | collective-permute-done | bytes 524320 | tf_op jit(solution)/shard_map/while/body/eval_jaxpr/ppermute | solution.py:10
  403.2 6.1 %collective-permute-start = (f32[4,256,128]{2,1,0:T(8,128)}, f32[4,256,128]{2,1,0:T(8,128)S(1)}, u32[]{:S(2)}, u32[]{:S(2)}) collective-permute-start(f32[4,256,128]{2,1,0:T(8,128)} %get-tuple-element.463), channel_id=1, source_target_pairs={{0,1},{1,2},{2,3},{3,4},{4,5},{5,6},{6,7},{8,9},{9,10},{10,11},{11... | collective-permute-start | bytes 1572872 | tf_op jit(solution)/shard_map/while/body/eval_jaxpr/ppermute | solution.py:10
  409.3 6.8 %collective-permute-done = f32[4,256,128]{2,1,0:T(8,128)S(1)} collective-permute-done((f32[4,256,128]{2,1,0:T(8,128)}, f32[4,256,128]{2,1,0:T(8,128)S(1)}, u32[]{:S(2)}, u32[]{:S(2)}) %collective-permute-start) | collective-permute-done | bytes 524320 | tf_op jit(solution)/shard_map/while/body/eval_jaxpr/ppermute | solution.py:10
  417.0 1.9 copy.11
  418.9 5.1 convolution_bitcast_fusion.1
  425.0 102.5 %all-to-all-start = ((f32[8,4,16,512]{3,2,1,0:T(8,128)}), f32[8,4,16,512]{3,2,1,0:T(8,128)S(1)}, u32[]{:S(2)}, u32[]{:S(2)}) async-start(f32[8,4,16,512]{3,2,1,0:T(8,128)} %copy.12), calls=%async_computation | async-start | bytes 2097152 | tf_op jit(solution)/shard_map/all_to_all | solution.py:21
  527.8 9.6 %all-to-all-done = f32[8,4,16,512]{3,2,1,0:T(8,128)S(1)} async-done(((f32[8,4,16,512]{3,2,1,0:T(8,128)}), f32[8,4,16,512]{3,2,1,0:T(8,128)S(1)}, u32[]{:S(2)}, u32[]{:S(2)}) %all-to-all-start) | async-done | bytes 1048608 | tf_op jit(solution)/shard_map/all_to_all | solution.py:21
  537.5 12.5 %collective-permute-start.2 = (f32[1,4,16,512]{3,2,1,0:T(8,128)S(1)}, f32[1,4,16,512]{3,2,1,0:T(8,128)S(1)}, u32[]{:S(2)}, u32[]{:S(2)}) collective-permute-start(f32[1,4,16,512]{3,2,1,0:T(8,128)S(1)} %bitcast.98), channel_id=1, source_target_pairs={{8,0},{16,8},{24,16},{32,24},{40,32},{48,40},{56,48},{64,56},{72,6... | collective-permute-start | bytes 393224 | tf_op jit(solution)/shard_map/ppermute | solution.py:33
  549.9 5.9 %collective-permute-start.1 = (f32[1,4,16,512]{3,2,1,0:T(8,128)S(1)}, f32[1,4,16,512]{3,2,1,0:T(8,128)S(1)}, u32[]{:S(2)}, u32[]{:S(2)}) collective-permute-start(f32[1,4,16,512]{3,2,1,0:T(8,128)S(1)} %bitcast.99), channel_id=1, source_target_pairs={{0,8},{8,16},{16,24},{24,32},{32,40},{40,48},{48,56},{56,64},{64,7... | collective-permute-start | bytes 393224 | tf_op jit(solution)/shard_map/ppermute | solution.py:30
  (116 shorter events, 88.6 us)
Async XLA Ops:
  3.2 17.3 %collective-permute-start = (f32[4,256,128]{2,1,0:T(8,128)}, f32[4,256,128]{2,1,0:T(8,128)S(1)}, u32[]{:S(2)}, u32[]{:S(2)}) collective-permute-start(f32[4,256,128]{2,1,0:T(8,128)} %get-tuple-element.463), channel_id=1, source_target_pairs={{0,1},{1,2},{2,3},{3,4},{4,5},{5,6},{6,7},{8,9},{9,10},{10,11},{11... | collective-permute-start | bytes 1572872 | tf_op jit(solution)/shard_map/while/body/eval_jaxpr/ppermute | solution.py:10
  21.3 16.4 %collective-permute-start = (f32[4,256,128]{2,1,0:T(8,128)}, f32[4,256,128]{2,1,0:T(8,128)S(1)}, u32[]{:S(2)}, u32[]{:S(2)}) collective-permute-start(f32[4,256,128]{2,1,0:T(8,128)} %get-tuple-element.463), channel_id=1, source_target_pairs={{0,1},{1,2},{2,3},{3,4},{4,5},{5,6},{6,7},{8,9},{9,10},{10,11},{11... | collective-permute-start | bytes 1572872 | tf_op jit(solution)/shard_map/while/body/eval_jaxpr/ppermute | solution.py:10
  38.6 74.2 %collective-permute-start = (f32[4,256,128]{2,1,0:T(8,128)}, f32[4,256,128]{2,1,0:T(8,128)S(1)}, u32[]{:S(2)}, u32[]{:S(2)}) collective-permute-start(f32[4,256,128]{2,1,0:T(8,128)} %get-tuple-element.463), channel_id=1, source_target_pairs={{0,1},{1,2},{2,3},{3,4},{4,5},{5,6},{6,7},{8,9},{9,10},{10,11},{11... | collective-permute-start | bytes 1572872 | tf_op jit(solution)/shard_map/while/body/eval_jaxpr/ppermute | solution.py:10
  146.6 15.3 %collective-permute-start = (f32[4,256,128]{2,1,0:T(8,128)}, f32[4,256,128]{2,1,0:T(8,128)S(1)}, u32[]{:S(2)}, u32[]{:S(2)}) collective-permute-start(f32[4,256,128]{2,1,0:T(8,128)} %get-tuple-element.463), channel_id=1, source_target_pairs={{0,1},{1,2},{2,3},{3,4},{4,5},{5,6},{6,7},{8,9},{9,10},{10,11},{11... | collective-permute-start | bytes 1572872 | tf_op jit(solution)/shard_map/while/body/eval_jaxpr/ppermute | solution.py:10
  195.6 14.4 %collective-permute-start = (f32[4,256,128]{2,1,0:T(8,128)}, f32[4,256,128]{2,1,0:T(8,128)S(1)}, u32[]{:S(2)}, u32[]{:S(2)}) collective-permute-start(f32[4,256,128]{2,1,0:T(8,128)} %get-tuple-element.463), channel_id=1, source_target_pairs={{0,1},{1,2},{2,3},{3,4},{4,5},{5,6},{6,7},{8,9},{9,10},{10,11},{11... | collective-permute-start | bytes 1572872 | tf_op jit(solution)/shard_map/while/body/eval_jaxpr/ppermute | solution.py:10
  243.8 13.5 %collective-permute-start = (f32[4,256,128]{2,1,0:T(8,128)}, f32[4,256,128]{2,1,0:T(8,128)S(1)}, u32[]{:S(2)}, u32[]{:S(2)}) collective-permute-start(f32[4,256,128]{2,1,0:T(8,128)} %get-tuple-element.463), channel_id=1, source_target_pairs={{0,1},{1,2},{2,3},{3,4},{4,5},{5,6},{6,7},{8,9},{9,10},{10,11},{11... | collective-permute-start | bytes 1572872 | tf_op jit(solution)/shard_map/while/body/eval_jaxpr/ppermute | solution.py:10
  291.1 12.5 %collective-permute-start = (f32[4,256,128]{2,1,0:T(8,128)}, f32[4,256,128]{2,1,0:T(8,128)S(1)}, u32[]{:S(2)}, u32[]{:S(2)}) collective-permute-start(f32[4,256,128]{2,1,0:T(8,128)} %get-tuple-element.463), channel_id=1, source_target_pairs={{0,1},{1,2},{2,3},{3,4},{4,5},{5,6},{6,7},{8,9},{9,10},{10,11},{11... | collective-permute-start | bytes 1572872 | tf_op jit(solution)/shard_map/while/body/eval_jaxpr/ppermute | solution.py:10
  304.4 40.8 %collective-permute-start = (f32[4,256,128]{2,1,0:T(8,128)}, f32[4,256,128]{2,1,0:T(8,128)S(1)}, u32[]{:S(2)}, u32[]{:S(2)}) collective-permute-start(f32[4,256,128]{2,1,0:T(8,128)} %get-tuple-element.463), channel_id=1, source_target_pairs={{0,1},{1,2},{2,3},{3,4},{4,5},{5,6},{6,7},{8,9},{9,10},{10,11},{11... | collective-permute-start | bytes 1572872 | tf_op jit(solution)/shard_map/while/body/eval_jaxpr/ppermute | solution.py:10
  346.1 12.5 %collective-permute-start = (f32[4,256,128]{2,1,0:T(8,128)}, f32[4,256,128]{2,1,0:T(8,128)S(1)}, u32[]{:S(2)}, u32[]{:S(2)}) collective-permute-start(f32[4,256,128]{2,1,0:T(8,128)} %get-tuple-element.463), channel_id=1, source_target_pairs={{0,1},{1,2},{2,3},{3,4},{4,5},{5,6},{6,7},{8,9},{9,10},{10,11},{11... | collective-permute-start | bytes 1572872 | tf_op jit(solution)/shard_map/while/body/eval_jaxpr/ppermute | solution.py:10
  359.4 43.0 %collective-permute-start = (f32[4,256,128]{2,1,0:T(8,128)}, f32[4,256,128]{2,1,0:T(8,128)S(1)}, u32[]{:S(2)}, u32[]{:S(2)}) collective-permute-start(f32[4,256,128]{2,1,0:T(8,128)} %get-tuple-element.463), channel_id=1, source_target_pairs={{0,1},{1,2},{2,3},{3,4},{4,5},{5,6},{6,7},{8,9},{9,10},{10,11},{11... | collective-permute-start | bytes 1572872 | tf_op jit(solution)/shard_map/while/body/eval_jaxpr/ppermute | solution.py:10
  403.2 12.9 %collective-permute-start = (f32[4,256,128]{2,1,0:T(8,128)}, f32[4,256,128]{2,1,0:T(8,128)S(1)}, u32[]{:S(2)}, u32[]{:S(2)}) collective-permute-start(f32[4,256,128]{2,1,0:T(8,128)} %get-tuple-element.463), channel_id=1, source_target_pairs={{0,1},{1,2},{2,3},{3,4},{4,5},{5,6},{6,7},{8,9},{9,10},{10,11},{11... | collective-permute-start | bytes 1572872 | tf_op jit(solution)/shard_map/while/body/eval_jaxpr/ppermute | solution.py:10
  424.0 103.5 %copy-start.1 = (s32[32,4]{0,1:T(4,128)S(1)}, s32[32,4]{0,1:T(4,128)}, u32[]{:S(2)}) copy-start(s32[32,4]{0,1:T(4,128)} %param.17) | copy-start | bytes 1540
  425.0 112.3 %all-to-all-start = ((f32[8,4,16,512]{3,2,1,0:T(8,128)}), f32[8,4,16,512]{3,2,1,0:T(8,128)S(1)}, u32[]{:S(2)}, u32[]{:S(2)}) async-start(f32[8,4,16,512]{3,2,1,0:T(8,128)} %copy.12), calls=%async_computation | async-start | bytes 2097152 | tf_op jit(solution)/shard_map/all_to_all | solution.py:21
  527.7 31.4 %copy-start = (f32[1,4,16,512]{3,2,1,0:T(8,128)S(1)}, f32[1,4,16,512]{3,2,1,0:T(8,128)}, u32[]{:S(2)}) copy-start(f32[1,4,16,512]{3,2,1,0:T(8,128)} %param.16) | copy-start | bytes 393220
  537.5 19.2 %collective-permute-start.2 = (f32[1,4,16,512]{3,2,1,0:T(8,128)S(1)}, f32[1,4,16,512]{3,2,1,0:T(8,128)S(1)}, u32[]{:S(2)}, u32[]{:S(2)}) collective-permute-start(f32[1,4,16,512]{3,2,1,0:T(8,128)S(1)} %bitcast.98), channel_id=1, source_target_pairs={{8,0},{16,8},{24,16},{32,24},{40,32},{48,40},{56,48},{64,56},{72,6... | collective-permute-start | bytes 393224 | tf_op jit(solution)/shard_map/ppermute | solution.py:33
  549.9 7.8 %collective-permute-start.1 = (f32[1,4,16,512]{3,2,1,0:T(8,128)S(1)}, f32[1,4,16,512]{3,2,1,0:T(8,128)S(1)}, u32[]{:S(2)}, u32[]{:S(2)}) collective-permute-start(f32[1,4,16,512]{3,2,1,0:T(8,128)S(1)} %bitcast.99), channel_id=1, source_target_pairs={{0,8},{8,16},{16,24},{24,32},{32,40},{40,48},{48,56},{56,64},{64,7... | collective-permute-start | bytes 393224 | tf_op jit(solution)/shard_map/ppermute | solution.py:30
where the time goes:
time: 566 us; the launch traced here: 560 us
  starting transfers between devices  219 us (39%)
  waiting for transfers between devices  186 us (33%)
  matrix products  91.6 us (16%)
  local copies, waits for them, and re-layouts  31.9 us (6%)
  loops' own time  30.5 us (5%)
    ppermute x11, waiting for transfers between devices, from_behind(): lax.ppermute(value, axis, [(source, source + steps) for source in range(f...  174 us
    all_to_all x1, starting transfers between devices, sent_and_summed(): parts = lax.all_to_all(in_blocks(value, dim, size), axis, 0, 0, tiled=True)  102 us
    ppermute x11, starting transfers between devices, from_behind(): lax.ppermute(value, axis, [(source, source + steps) for source in range(f...  98.4 us
    dot_general x48, matrix products, substitute(): jnp.dot(factor_row[band], source, precision=lax.Precision.HIGHEST)  64.1 us
    another operation x4, loops' own time, solve(): lax.fori_loop(jnp.int32(0), jnp.int32(brows), substitute, extended)  30.2 us
    dot_general x16, matrix products, substitute(): solved_row = jnp.dot(inverse, running, precision=lax.Precision.HIGHEST)  21.3 us
    ppermute x1, starting transfers between devices, padded(): lax.ppermute(lax.slice_in_dim(block, 0, width, axis=dim), axis, backward)  12.5 us
  transfers between devices with their start and end apart: 14, of which 14 were waited for; matrix products, arithmetic and copies ran while one was open for 0% of the time, Pallas kernels for 0%

commit v1 on v0

v1 whole, which is shorter than its diff:
```python
import functools

import jax
import jax.numpy as jnp
from jax import lax
from jax.experimental import pallas as pl
from jax.experimental.pallas import tpu as pltpu
from jax.sharding import PartitionSpec as P

MESH = pl.DeviceIdType.MESH
F32 = jnp.float32
BF16 = jnp.bfloat16
CHUNK = 16
NT = (((1,), (1,)), ((), ()))
NN = (((1,), (0,)), ((), ()))


def split(value):
    high = value.astype(BF16)
    low = (value - high.astype(F32)).astype(BF16)
    return high, low


def dot(a, b, dims):
    return lax.dot_general(a, b, dims, preferred_element_type=F32)


def dot3(ah, al, bh, bl, dims=NT):
    return dot(ah, bh, dims) + dot(ah, bl, dims) + dot(al, bh, dims)


def kernel(
    subs,
    rows,
    factor,
    inverse,
    offsets,
    coupling,
    interface,
    tile_ids,
    out,
    lh,
    ll,
    ih,
    il,
    yt,
    yh,
    yl,
    wh,
    wl,
    arrived,
    gpart,
    grecv,
    gsum,
    nearby,
    chain_send,
    chain_recv,
    gram_send,
    gram_recv,
    near_send,
    near_recv,
):
    sub = lax.axis_index("sub")
    row = lax.axis_index("row")
    brows, kband, block, _ = factor.shape
    cols = coupling.shape[1]
    chunks = cols // CHUNK
    tiles, share, _ = interface.shape
    tile = cols // tiles

    nearby[...] = jnp.zeros_like(nearby)

    barrier = pltpu.get_barrier_semaphore()
    for step in range(1, rows):
        pl.semaphore_signal(
            barrier, inc=1, device_id=(sub, lax.rem(row + step, rows)), device_id_type=MESH
        )
    has_left = sub > 0
    has_right = sub < subs - 1

    @pl.when(has_left)
    def _():
        pl.semaphore_signal(barrier, inc=1, device_id=(sub - 1, row), device_id_type=MESH)

    @pl.when(has_right)
    def _():
        pl.semaphore_signal(barrier, inc=1, device_id=(sub + 1, row), device_id_type=MESH)

    for r in range(brows):
        for offset in range(1, brows + 1):
            value = jnp.zeros((block, block), F32)
            for band in range(kband):
                if band + 1 <= offset <= band + 2:
                    value = jnp.where(offsets[r, band] == offset, factor[r, band], value)
            high, low = split(value)
            lh[r * brows + offset - 1] = high
            ll[r * brows + offset - 1] = low
        high, low = split(inverse[r])
        ih[r] = high
        il[r] = low

    def span(r):
        return slice(r * block, (r + 1) * block)

    for r in range(brows):
        right = coupling[span(r), :].T
        for offset in range(1, r + 1):
            s = span(r - offset)
            i = r * brows + offset - 1
            right = right - dot3(yh[:, s], yl[:, s], lh[i], ll[i])
        high, low = split(right)
        solved = dot3(high, low, ih[r], il[r])
        yt[:, span(r)] = solved
        high, low = split(solved)
        yh[:, span(r)] = high
        yl[:, span(r)] = low

    pl.semaphore_wait(barrier, rows - 1 + has_left.astype(jnp.int32) + has_right.astype(jnp.int32))

    following = lax.rem(row + 1, rows)

    def rows_of(c):
        return pl.ds(pl.multiple_of(c * CHUNK, CHUNK), CHUNK)

    def chain_copy(c):
        return pltpu.make_async_remote_copy(
            src_ref=yt.at[rows_of(c)],
            dst_ref=arrived.at[rows_of(c)],
            send_sem=chain_send.at[c],
            recv_sem=chain_recv.at[c],
            device_id=(sub, following),
            device_id_type=MESH,
        )

    @pl.when(row == 0)
    def _():
        @pl.loop(0, chunks)
        def _(c):
            chain_copy(c).start()

    @pl.when(row > 0)
    def _():
        @pl.loop(0, brows)
        def _(b):
            k = pl.ds(pl.multiple_of(b * block, block), block)
            for r in range(brows):
                i = jnp.clip(r * brows + brows + r - b - 1, 0, brows * brows - 1)
                placed = lh[i].astype(F32) + ll[i].astype(F32)
                right = jnp.where(b >= r, -placed.T, 0.0)
                for offset in range(1, r + 1):
                    s = span(r - offset)
                    j = r * brows + offset - 1
                    right = right - dot3(wh[k, s], wl[k, s], lh[j], ll[j])
                high, low = split(right)
                solved = dot3(high, low, ih[r], il[r])
                high, low = split(solved)
                wh[k, span(r)] = high
                wl[k, span(r)] = low

        @pl.loop(0, chunks)
        def _(c):
            chain_copy(c).wait_recv()
            here = rows_of(c)
            high, low = split(arrived[here, :])
            both = dot(jnp.concatenate([high, low], 0), wh[...], NN)
            value = yt[here, :] + (both[:CHUNK] + (both[CHUNK:] + dot(high, wl[...], NN)))
            yt[here, :] = value

            @pl.when(row < rows - 1)
            def _():
                chain_copy(c).start()

            high, low = split(value)
            yh[here, :] = high
            yl[here, :] = low

    half = cols // 2
    for part in range(2):
        mine = pl.ds(part * half, half)
        gram = dot3(yh[mine, :], yl[mine, :], yh[...], yl[...])
        for k in range(half // tile):
            for r in range(rows):
                at = k * tile + r * share
                gpart[r, part * (half // tile) + k] = gram[at : at + share]

    def gram_copy(step):
        to = lax.rem(row + step, rows)
        return pltpu.make_async_remote_copy(
            src_ref=gpart.at[to],
            dst_ref=grecv.at[step],
            send_sem=gram_send.at[step],
            recv_sem=gram_recv.at[step],
            device_id=(sub, to),
            device_id_type=MESH,
        )

    for step in range(1, rows):
        gram_copy(step).start()
    total = gpart[row]
    for step in range(1, rows):
        gram_copy(step).wait_recv()
        total = total + grecv[step]
    gsum[...] = total

    def near_copy(side):
        return pltpu.make_async_remote_copy(
            src_ref=gsum,
            dst_ref=nearby.at[side],
            send_sem=near_send.at[side],
            recv_sem=near_recv.at[side],
            device_id=(sub + 1 if side == 0 else sub - 1, row),
            device_id_type=MESH,
        )

    @pl.when(has_right)
    def _():
        near_copy(0).start()

    @pl.when(has_left)
    def _():
        near_copy(1).start()

    left = jnp.maximum(sub - 1, 0)
    right = jnp.minimum(sub + 1, subs - 1)

    @pl.when(has_left)
    def _():
        near_copy(0).wait_recv()

    @pl.when(has_right)
    def _():
        near_copy(1).wait_recv()

    result = interface[...] - gsum[...]
    for side, (other, exists) in enumerate(((left, has_left), (right, has_right))):
        match = [
            [
                jnp.where((tile_ids[sub, i] == tile_ids[other, k]) & exists, 1.0, 0.0)
                for k in range(tiles)
            ]
            for i in range(tiles)
        ]
        gram = nearby[side]
        taken = []
        for i in range(tiles):
            across = sum(match[i][k] * gram[k] for k in range(tiles))
            pieces = [
                sum(match[j][m] * across[:, m * tile : (m + 1) * tile] for m in range(tiles))
                for j in range(tiles)
            ]
            taken.append(jnp.concatenate(pieces, 1))
        result = result - jnp.stack(taken)
    out[...] = result

    @pl.when(row < rows - 1)
    def _():
        @pl.loop(0, chunks)
        def _(c):
            chain_copy(c).wait_send()

    for step in range(1, rows):
        gram_copy(step).wait_send()

    @pl.when(has_right)
    def _():
        near_copy(0).wait_send()

    @pl.when(has_left)
    def _():
        near_copy(1).wait_send()


def shards(
    subs, rows, factor_blocks, block_inverses, band_offsets, coupling, interface_block, tile_ids
):
    brows, _, block, _ = factor_blocks.shape[1:]
    height, cols = coupling.shape[1:]
    tiles, share, _ = interface_block.shape[1:]
    vmem = pl.BlockSpec(memory_space=pltpu.VMEM)
    smem = pl.BlockSpec(memory_space=pltpu.SMEM)
    scratch = [
        pltpu.VMEM((brows * brows, block, block), BF16),
        pltpu.VMEM((brows * brows, block, block), BF16),
        pltpu.VMEM((brows, block, block), BF16),
        pltpu.VMEM((brows, block, block), BF16),
        pltpu.VMEM((cols, height), F32),
        pltpu.VMEM((cols, height), BF16),
        pltpu.VMEM((cols, height), BF16),
        pltpu.VMEM((height, height), BF16),
        pltpu.VMEM((height, height), BF16),
        pltpu.VMEM((cols, height), F32),
        pltpu.VMEM((rows, tiles, share, cols), F32),
        pltpu.VMEM((rows, tiles, share, cols), F32),
        pltpu.VMEM((tiles, share, cols), F32),
        pltpu.VMEM((2, tiles, share, cols), F32),
        pltpu.SemaphoreType.DMA((cols // CHUNK,)),
        pltpu.SemaphoreType.DMA((cols // CHUNK,)),
        pltpu.SemaphoreType.DMA((rows,)),
        pltpu.SemaphoreType.DMA((rows,)),
        pltpu.SemaphoreType.DMA((2,)),
        pltpu.SemaphoreType.DMA((2,)),
    ]
    result = pl.pallas_call(
        functools.partial(kernel, subs, rows),
        out_shape=jax.ShapeDtypeStruct((tiles, share, cols), F32),
        in_specs=[vmem, vmem, smem, vmem, vmem, smem],
        out_specs=vmem,
        scratch_shapes=scratch,
        compiler_params=pltpu.CompilerParams(
            collective_id=0, has_side_effects=True, vmem_limit_bytes=60 * 1024 * 1024
        ),
    )(
        factor_blocks[0],
        block_inverses[0],
        band_offsets[0],
        coupling[0],
        interface_block[0],
        tile_ids,
    )
    return result[None]


def solution(mesh):
    return jax.shard_map(
        functools.partial(shards, mesh.shape["sub"], mesh.shape["row"]),
        mesh=mesh,
        in_specs=(
            P("sub", "row", None, None, None),
            P("sub", "row", None, None),
            P("sub", "row", None),
            P("sub", "row", None),
            P("sub", None, "row", None),
            P(),
        ),
        out_specs=P("sub", None, "row", None),
        check_vma=False,
    )
```

time: 566 us -> 121 us (0.21)
  starting transfers between devices: 219 us -> 0 us
  waiting for transfers between devices: 186 us -> 0 us
  Pallas kernels: 0 us -> 115 us
  matrix products: 91.6 us -> 0 us
  loops' own time: 30.5 us -> 0 us
  local copies, waits for them, and re-layouts: 31.9 us -> 4.28 us
    ppermute x13 -> x0, waiting for transfers between devices: 176 us -> none  [the longest x11 174 us: from_behind(): lax.ppermute(value, axis, [(source, source + steps) for source in range(f...]
    ppermute x13 -> x0, starting transfers between devices: 117 us -> none  [the longest x11 98.4 us: from_behind(): lax.ppermute(value, axis, [(source, source + steps) for source in range(f...]
    pallas_call x0 -> x1, Pallas kernels: none -> 115 us  [shards(): pl.pallas_call(functools.partial(kernel, subs, rows), out_shape=jax.Shape...]
    all_to_all x1 -> x0, starting transfers between devices: 102 us -> none  [sent_and_summed(): parts = lax.all_to_all(in_blocks(value, dim, size), axis, 0, 0, tiled=True)]
    dot_general x67 -> x0, matrix products: 91.6 us -> none  [the longest x48 64.1 us: substitute(): jnp.dot(factor_row[band], source, precision=lax.Precision.HIGHEST)]
    another operation x16 -> x0, loops' own time: 30.5 us -> none  [the longest x4 30.2 us: solve(): lax.fori_loop(jnp.int32(0), jnp.int32(brows), substitute, extended)]
    slice x16 -> x0, local copies, waits for them, and re-layouts: 10.3 us -> none  [substitute(): source_index = brows + row_block - offset_row[band]]
    all_to_all x1 -> x0, waiting for transfers between devices: 9.62 us -> none  [sent_and_summed(): parts = lax.all_to_all(in_blocks(value, dim, size), axis, 0, 0, tiled=True)]
  transfers between devices with their start and end apart: 14 -> 0, of which waited for: 14 -> 0; matrix products, arithmetic and copies ran while one was open for 0% -> 0% of each run, Pallas kernels for 0% -> 0%
where the time goes in v1:
time: 121 us; the launch traced here: 119 us
  Pallas kernels  115 us (95%)
  local copies, waits for them, and re-layouts  4.28 us (4%)
    pallas_call x1, Pallas kernels, shards(): pl.pallas_call(functools.partial(kernel, subs, rows), out_shape=jax.Shape...  115 us
    unnamed x3, local copies, waits for them, and re-layouts  4.28 us

profile of v1, /device:TPU:107, one launch (start us, length us, event | category | flops | bytes accessed | tf_op | source)
XLA Modules:
  0.0 119.4 jit_solution(7781195195806237385)
XLA Ops:
  0.0 1.3 %copy.7 = s32[1,4,3]{2,1,0:T(4,128)} copy(s32[1,4,3]{1,0,2:T(1,128)} %param.8) | data formatting | bytes 96 | tf_op args[2]
  1.3 1.4 %copy.8.tile_ids = s32[32,4]{1,0:T(8,128)} copy(s32[32,4]{0,1:T(4,128)} %param.11) | data formatting | bytes 1024 | tf_op args[5]
  2.7 115.1 %shard_map.64 = f32[4,16,512]{2,1,0:T(8,128)} custom-call(f32[4,3,256,256]{3,2,1,0:T(8,128)} %bitcast.6, f32[4,256,256]{2,1,0:T(8,128)} %bitcast.8, s32[4,3]{1,0:T(4,128)} %bitcast.11, f32[1024,512]{1,0:T(8,128)} %bitcast.7, f32[4,16,512]{2,1,0:T(8,128)} %bitcast.10, s32[32,4]{1,0:T(8,128)} %copy.8.tile_ids), custom_call_target="tpu_custom_call" | custom-call | tf_op jit(solution)/shard_map/pallas_call | solution.py:303
  117.8 1.6 %copy.10 = f32[1,4,16,512]{3,2,1,0:T(8,128)} copy(f32[1,4,16,512]{3,2,1,0:T(8,128)} %bitcast.9) | data formatting | bytes 262144

commit v2 on v1

v2 whole, which is shorter than its diff:
```python
import functools

import jax
import jax.numpy as jnp
from jax import lax
from jax.experimental import pallas as pl
from jax.experimental.pallas import tpu as pltpu
from jax.sharding import PartitionSpec as P

MESH = pl.DeviceIdType.MESH
F32 = jnp.float32
BF16 = jnp.bfloat16
CHUNK = 16
NT = (((1,), (1,)), ((), ()))
NN = (((1,), (0,)), ((), ()))


def split(value):
    high = value.astype(BF16)
    low = (value - high.astype(F32)).astype(BF16)
    return high, low


def dot(a, b, dims):
    return lax.dot_general(a, b, dims, preferred_element_type=F32)


def dot3(ah, al, bh, bl, dims=NT):
    return dot(ah, bh, dims) + dot(ah, bl, dims) + dot(al, bh, dims)


def kernel(
    subs,
    rows,
    factor_hbm,
    inverse_hbm,
    offsets,
    coupling_hbm,
    tile_ids,
    out,
    factor,
    inverse,
    coupling,
    nh,
    nl,
    ih,
    il,
    yt,
    yh,
    yl,
    wh,
    wl,
    arrived,
    gpart,
    grecv,
    gsum,
    nearby,
    load_sem,
    chain_send,
    chain_recv,
    gram_send,
    gram_recv,
    near_send,
    near_recv,
):
    sub = lax.axis_index("sub")
    row = lax.axis_index("row")
    brows, kband, block, _ = factor.shape
    height, cols = coupling.shape
    chunks = cols // CHUNK
    tiles = tile_ids.shape[0]
    tile = cols // tiles
    share = tile // rows
    odd = lax.rem(row, 2) == 1
    last = row == rows - 1

    loads = [
        pltpu.make_async_copy(source, target, load_sem.at[i])
        for i, (source, target) in enumerate(
            ((inverse_hbm, inverse), (factor_hbm, factor), (coupling_hbm, coupling))
        )
    ]
    for load in loads:
        load.start()

    nearby[...] = jnp.zeros_like(nearby)

    barrier = pltpu.get_barrier_semaphore()
    for step in range(1, rows):
        pl.semaphore_signal(
            barrier, inc=1, device_id=(sub, lax.rem(row + step, rows)), device_id_type=MESH
        )
    has_left = sub > 0
    has_right = sub < subs - 1

    @pl.when(has_left)
    def _():
        pl.semaphore_signal(barrier, inc=1, device_id=(sub - 1, row), device_id_type=MESH)

    @pl.when(has_right)
    def _():
        pl.semaphore_signal(barrier, inc=1, device_id=(sub + 1, row), device_id_type=MESH)

    def span(r):
        return slice(r * block, (r + 1) * block)

    def own(r):
        return slice(height + r * block, height + (r + 1) * block)

    def at_offset(r, offset):
        value = jnp.zeros((block, block), F32)
        for band in range(kband):
            if band + 1 <= offset <= band + 2:
                value = jnp.where(offsets[band, 0, r] == offset, factor[r, band], value)
        return value

    def local(r, offset):
        return r * (r - 1) // 2 + offset - 1

    loads[0].wait()
    for r in range(brows):
        high, low = split(inverse[r])
        ih[r] = high
        il[r] = low
    loads[1].wait()
    for r in range(1, brows):
        for offset in range(1, r + 1):
            high, low = split(at_offset(r, offset))
            high, low = split(dot3(ih[r], il[r], high, low, NN))
            nh[local(r, offset)] = high
            nl[local(r, offset)] = low

    loads[2].wait()
    for r in range(brows):
        high, low = split(coupling[span(r), :].T)
        solved = dot3(high, low, ih[r], il[r])
        for offset in range(r, 0, -1):
            s = own(r - offset)
            n = local(r, offset)
            solved = solved - dot3(yh[:, s], yl[:, s], nh[n], nl[n])
        yt[:, span(r)] = solved
        high, low = split(solved)
        yh[:, own(r)] = high
        yl[:, own(r)] = low

    pl.semaphore_wait(
        barrier, rows - 1 + has_left.astype(jnp.int32) + has_right.astype(jnp.int32)
    )

    following = lax.rem(row + 1, rows)

    def rows_of(c):
        return pl.ds(pl.multiple_of(c * CHUNK, CHUNK), CHUNK)

    def chain_copy(c):
        return pltpu.make_async_remote_copy(
            src_ref=yt.at[rows_of(c)],
            dst_ref=arrived.at[rows_of(c)],
            send_sem=chain_send.at[c],
            recv_sem=chain_recv.at[c],
            device_id=(sub, following),
            device_id_type=MESH,
        )

    def stage(q):
        return pl.ds(q * q, 2 * q + 1)

    def gram_copy(q, step):
        to = lax.rem(row + step, rows)
        return pltpu.make_async_remote_copy(
            src_ref=gpart.at[to, stage(q)],
            dst_ref=grecv.at[row // 2, stage(q)],
            send_sem=gram_send.at[q, step],
            recv_sem=gram_recv.at[q, row // 2],
            device_id=(sub, to),
            device_id_type=MESH,
        )

    def gram_stage(q):
        mine = slice(q * tile, (q + 1) * tile)
        upto = slice(0, (q + 1) * tile)
        high = yh[mine, :]
        both = dot(jnp.concatenate([high, yl[mine, :]], 0), yh[upto, :], NT)
        gram = both[:tile] + (both[tile:] + dot(high, yl[upto, :], NT))
        for l in range(q + 1):
            part = gram[:, l * tile : (l + 1) * tile]
            gpart[:, q * q + l] = part.reshape(rows, share, tile)
            if l < q:
                gpart[:, q * q + q + 1 + l] = part.T.reshape(rows, share, tile)
        for step in range(1, rows):
            gram_copy(q, step).start()
        grecv[row // 2, stage(q)] = gpart[row, stage(q)]

    @pl.when(row == 0)
    def _():
        @pl.loop(0, chunks)
        def _(c):
            chain_copy(c).start()

    @pl.when(row > 0)
    def _():
        for b in range(brows):
            for r in range(b + 1):
                high, low = split(-at_offset(r, brows + r - b).T)
                wh[span(b), span(r)] = high
                wl[span(b), span(r)] = low
        for b0 in range(0, brows, 2):
            k = slice(b0 * block, (b0 + 2) * block)
            for r in range(brows):
                solved = None
                first = max(r, b0)
                if first < b0 + 2:
                    part = slice(first * block, (b0 + 2) * block)
                    solved = dot3(wh[part, span(r)], wl[part, span(r)], ih[r], il[r])
                    if first > b0:
                        solved = jnp.concatenate(
                            [jnp.zeros(((first - b0) * block, block), F32), solved], 0
                        )
                for offset in range(r, 0, -1):
                    s = span(r - offset)
                    n = local(r, offset)
                    term = dot3(wh[k, s], wl[k, s], nh[n], nl[n])
                    solved = -term if solved is None else solved - term
                high, low = split(solved)
                wh[k, span(r)] = high
                wl[k, span(r)] = low

        @pl.loop(0, chunks)
        def _(c):
            chain_copy(c).wait_recv()
            here = rows_of(c)
            high, low = split(arrived[here, :])
            both = dot(jnp.concatenate([high, low], 0), wh[...], NN)
            value = yt[here, :] + (both[:CHUNK] + (both[CHUNK:] + dot(high, wl[...], NN)))
            yt[here, :] = value

            @pl.when(row < rows - 1)
            def _():
                chain_copy(c).start()

            yh[here, :height] = high
            yl[here, :height] = low
            high, low = split(value)
            yh[here, height:] = high
            yl[here, height:] = low

            for q in range(tiles - 1):
                @pl.when(last & (c == (q + 1) * (chunks // tiles) - 1))
                def _():
                    gram_stage(q)

    @pl.when(odd & (row < rows - 1))
    def _():
        for q in range(tiles - 1):
            gram_stage(q)

    @pl.when(odd)
    def _():
        gram_stage(tiles - 1)

    def near_copy(side, q):
        return pltpu.make_async_remote_copy(
            src_ref=gsum.at[stage(q)],
            dst_ref=nearby.at[side, stage(q)],
            send_sem=near_send.at[side, q],
            recv_sem=near_recv.at[side, q],
            device_id=(sub + 1 if side == 0 else sub - 1, row),
            device_id_type=MESH,
        )

    for q in range(tiles):
        for j in range(rows // 2):
            @pl.when(row != 2 * j + 1)
            def _():
                pltpu.make_async_remote_copy(
                    src_ref=gpart.at[0, stage(q)],
                    dst_ref=grecv.at[j, stage(q)],
                    send_sem=gram_send.at[q, 0],
                    recv_sem=gram_recv.at[q, j],
                    device_id=(sub, following),
                    device_id_type=MESH,
                ).wait_recv()
        total = grecv[0, stage(q)]
        for j in range(1, rows // 2):
            total = total + grecv[j, stage(q)]
        gsum[stage(q)] = total

        @pl.when(has_right)
        def _():
            near_copy(0, q).start()

        @pl.when(has_left)
        def _():
            near_copy(1, q).start()

    for q in range(tiles):
        @pl.when(has_left)
        def _():
            near_copy(0, q).wait_recv()

        @pl.when(has_right)
        def _():
            near_copy(1, q).wait_recv()

    def index(k, l):
        return k * k + l if k >= l else l * l + l + 1 + k

    left = jnp.maximum(sub - 1, 0)
    right = jnp.minimum(sub + 1, subs - 1)
    matches = [
        [
            [
                jnp.where((tile_ids[i, sub] == tile_ids[k, other]) & exists, 1.0, 0.0)
                for k in range(tiles)
            ]
            for i in range(tiles)
        ]
        for other, exists in ((left, has_left), (right, has_right))
    ]
    for i in range(tiles):
        across = [
            [sum(match[i][k] * nearby[side, index(k, m)] for k in range(tiles)) for m in range(tiles)]
            for side, match in enumerate(matches)
        ]
        for j in range(tiles):
            value = gsum[index(i, j)]
            for match, taken in zip(matches, across):
                value = value + sum(match[j][m] * taken[m] for m in range(tiles))
            out[i, :, j * tile : (j + 1) * tile] = value

    @pl.when(row < rows - 1)
    def _():
        @pl.loop(0, chunks)
        def _(c):
            chain_copy(c).wait_send()

    @pl.when(odd)
    def _():
        for q in range(tiles):
            for step in range(1, rows):
                gram_copy(q, step).wait_send()

    for q in range(tiles):
        @pl.when(has_right)
        def _():
            near_copy(0, q).wait_send()

        @pl.when(has_left)
        def _():
            near_copy(1, q).wait_send()


def shards(
    subs, rows, factor_blocks, block_inverses, band_offsets, coupling, interface_block, tile_ids
):
    brows, kband, block, _ = factor_blocks.shape[1:]
    height, cols = coupling.shape[1:]
    tiles, share, _ = interface_block.shape[1:]
    tile = cols // tiles
    locals_ = brows * (brows - 1) // 2
    hbm = pl.BlockSpec(memory_space=pl.ANY)
    vmem = pl.BlockSpec(memory_space=pltpu.VMEM)
    smem = pl.BlockSpec(memory_space=pltpu.SMEM)
    dma = pltpu.SemaphoreType.DMA
    scratch = [
        pltpu.VMEM((brows, kband, block, block), F32),
        pltpu.VMEM((brows, block, block), F32),
        pltpu.VMEM((height, cols), F32),
        pltpu.VMEM((locals_, block, block), BF16),
        pltpu.VMEM((locals_, block, block), BF16),
        pltpu.VMEM((brows, block, block), BF16),
        pltpu.VMEM((brows, block, block), BF16),
        pltpu.VMEM((cols, height), F32),
        pltpu.VMEM((cols, 2 * height), BF16),
        pltpu.VMEM((cols, 2 * height), BF16),
        pltpu.VMEM((height, height), BF16),
        pltpu.VMEM((height, height), BF16),
        pltpu.VMEM((cols, height), F32),
        pltpu.VMEM((rows, tiles * tiles, share, tile), F32),
        pltpu.VMEM((rows // 2, tiles * tiles, share, tile), F32),
        pltpu.VMEM((tiles * tiles, share, tile), F32),
        pltpu.VMEM((2, tiles * tiles, share, tile), F32),
        dma((3,)),
        dma((cols // CHUNK,)),
        dma((cols // CHUNK,)),
        dma((tiles, rows)),
        dma((tiles, rows // 2)),
        dma((2, tiles)),
        dma((2, tiles)),
    ]
    contribution = pl.pallas_call(
        functools.partial(kernel, subs, rows),
        out_shape=jax.ShapeDtypeStruct((tiles, share, cols), F32),
        in_specs=[hbm, hbm, smem, hbm, smem],
        out_specs=vmem,
        scratch_shapes=scratch,
        compiler_params=pltpu.CompilerParams(
            collective_id=0, has_side_effects=True, vmem_limit_bytes=60 * 1024 * 1024
        ),
    )(
        factor_blocks[0],
        block_inverses[0],
        jnp.transpose(band_offsets, (2, 0, 1)),
        coupling[0],
        tile_ids.T,
    )
    return interface_block - contribution[None]


def solution(mesh):
    return jax.shard_map(
        functools.partial(shards, mesh.shape["sub"], mesh.shape["row"]),
        mesh=mesh,
        in_specs=(
            P("sub", "row", None, None, None),
            P("sub", "row", None, None),
            P("sub", "row", None),
            P("sub", "row", None),
            P("sub", None, "row", None),
            P(),
        ),
        out_specs=P("sub", None, "row", None),
        check_vma=False,
    )
```

time: 121 us -> 107 us (0.88); the launches traced: 119 us -> 107 us
  Pallas kernels: 115 us -> 105 us
  local copies, waits for them, and re-layouts: 4.28 us -> 0.01 us
  other arithmetic: 0 us -> 1.58 us
    pallas_call x1, Pallas kernels: 115 us -> 105 us  [shards(): pl.pallas_call(functools.partial(kernel, subs, rows), out_shape=jax.Shape...]
    unnamed x3 -> x2, local copies, waits for them, and re-layouts: 4.28 us -> 0.01 us
    sub x0 -> x1, other arithmetic: none -> 1.58 us  [shards(): return interface_block - contribution[None]]
where the time goes in v2:
time: 107 us
  Pallas kernels  105 us (98%)
  other arithmetic  1.58 us (1%)
    pallas_call x1, Pallas kernels, shards(): pl.pallas_call(functools.partial(kernel, subs, rows), out_shape=jax.Shape...  105 us

profile of v2, /device:TPU:107, one launch (start us, length us, event | category | flops | bytes accessed | tf_op | source)
XLA Modules:
  0.0 106.9 jit_solution(11076132211906428444)
XLA Ops:
  0.0 0.0 copy-start
  0.0 105.3 %shard_map.64 = f32[4,16,512]{2,1,0:T(8,128)} custom-call(f32[4,3,256,256]{3,2,1,0:T(8,128)} %bitcast.7, f32[4,256,256]{2,1,0:T(8,128)} %bitcast.9, s32[3,1,4]{2,1,0:T(1,128)} %bitcast.11, f32[1024,512]{1,0:T(8,128)} %bitcast.8, s32[4,32]{1,0:T(4,128)} %bitcast.10), custom_call_target="tpu_custom_call" | custom-call | tf_op jit(solution)/shard_map/pallas_call | solution.py:391
  105.4 0.0 copy-done
  105.4 1.6 %bitcast_subtract_fusion = f32[1,4,16,512]{3,2,1,0:T(8,128)} fusion(f32[1,4,16,512]{3,2,1,0:T(8,128)S(1)} %copy-done, f32[4,16,512]{2,1,0:T(8,128)} %shard_map.64), kind=kLoop, calls=%fused_computation | loop fusion | flops 32768 | bytes 393216 | tf_op jit(solution)/shard_map/sub | solution.py:407
Async XLA Ops:
  0.0 105.4 %copy-start = (f32[1,4,16,512]{3,2,1,0:T(8,128)S(1)}, f32[1,4,16,512]{3,2,1,0:T(8,128)}, u32[]{:S(2)}) copy-start(f32[1,4,16,512]{3,2,1,0:T(8,128)} %param.10) | copy-start | bytes 393220

commit v3 on v2

--- a/solution.py
+++ b/solution.py
@@ -54,14 +54,19 @@
     gpart,
     grecv,
     gsum,
+    perm,
+    shared,
     nearby,
     load_sem,
     chain_send,
     chain_recv,
     gram_send,
     gram_recv,
+    stage_send,
+    stage_recv,
     near_send,
     near_recv,
+    go,
 ):
     sub = lax.axis_index("sub")
     row = lax.axis_index("row")
@@ -71,7 +76,13 @@
     tiles = tile_ids.shape[0]
     tile = cols // tiles
     share = tile // rows
-    odd = lax.rem(row, 2) == 1
+    half = rows // 2
+    parity = lax.rem(row, 2)
+    odd = parity == 1
+    mine = row // 2
+    piece = tiles * share
+    lanes = 2 * piece
+    parts = cols // lanes
     last = row == rows - 1
 
     loads = [
@@ -132,7 +143,11 @@
 
     loads[2].wait()
     for r in range(brows):
-        high, low = split(coupling[span(r), :].T)
+        natural = coupling[span(r), :].T
+        order = [
+            k * tile + (2 * j + p) * share for p in range(2) for j in range(half) for k in range(tiles)
+        ]
+        high, low = split(jnp.concatenate([natural[n : n + share] for n in order], 0))
         solved = dot3(high, low, ih[r], il[r])
         for offset in range(r, 0, -1):
             s = own(r - offset)
@@ -162,40 +177,74 @@
             device_id_type=MESH,
         )
 
-    def stage(q):
-        return pl.ds(q * q, 2 * q + 1)
-
-    def gram_copy(q, step):
-        to = lax.rem(row + step, rows)
+    def gram_of(start, count, part, width, depth):
+        high = yh[start : start + count, depth:]
+        low = yl[start : start + count, depth:]
+        at = slice(part * lanes, part * lanes + width)
+        both = dot(jnp.concatenate([high, low], 0), yh[at, depth:], NT)
+        return both[:count] + (both[count:] + dot(high, yl[at, depth:], NT))
+
+    def keep(gram, slot, part):
+        for j in range(gram.shape[0] // piece):
+            for m in range(gram.shape[1] // lanes):
+                gpart[slot + j, part + m] = gram[
+                    j * piece : (j + 1) * piece, m * lanes : (m + 1) * lanes
+                ]
+
+    def gram_copy(step):
+        to = lax.rem(mine + step, half)
         return pltpu.make_async_remote_copy(
-            src_ref=gpart.at[to, stage(q)],
-            dst_ref=grecv.at[row // 2, stage(q)],
-            send_sem=gram_send.at[q, step],
-            recv_sem=gram_recv.at[q, row // 2],
-            device_id=(sub, to),
+            src_ref=gpart.at[to],
+            dst_ref=grecv.at[mine],
+            send_sem=gram_send.at[step],
+            recv_sem=gram_recv.at[mine],
+            device_id=(sub, 2 * to + parity),
             device_id_type=MESH,
         )
 
+    def stage_copy(q, j):
+        even = j % 2 == 0
+        if even:
+            at = pl.ds(0, 2) if q == 1 else pl.ds(q, 1)
+        else:
+            first = (half + j // 2) // 2
+            at = pl.ds(0, q + 1) if q == first else pl.ds(q, 1)
+        return pltpu.make_async_remote_copy(
+            src_ref=gpart.at[j // 2 + (half if even else 0), at],
+            dst_ref=grecv.at[half if even else half - 1, at],
+            send_sem=stage_send.at[q, j],
+            recv_sem=stage_recv.at[q],
+            device_id=(sub, j),
+            device_id_type=MESH,
+        )
+
+    def targets(q):
+        evens = [] if q == 0 else list(range(0, rows, 2))
+        odds = [j for j in range(1, rows - 1, 2) if (half + j // 2) // 2 <= q]
+        return odds + evens
+
     def gram_stage(q):
-        mine = slice(q * tile, (q + 1) * tile)
-        upto = slice(0, (q + 1) * tile)
-        high = yh[mine, :]
-        both = dot(jnp.concatenate([high, yl[mine, :]], 0), yh[upto, :], NT)
-        gram = both[:tile] + (both[tile:] + dot(high, yl[upto, :], NT))
-        for l in range(q + 1):
-            part = gram[:, l * tile : (l + 1) * tile]
-            gpart[:, q * q + l] = part.reshape(rows, share, tile)
-            if l < q:
-                gpart[:, q * q + q + 1 + l] = part.T.reshape(rows, share, tile)
-        for step in range(1, rows):
-            gram_copy(q, step).start()
-        grecv[row // 2, stage(q)] = gpart[row, stage(q)]
+        own_rows = half * piece
+        if q == 1:
+            keep(gram_of(0, own_rows, 0, 2 * lanes, height), half, 0)
+        if q >= 2:
+            keep(gram_of(0, own_rows, q, lanes, height), half, q)
+        if q == 2:
+            keep(gram_of(own_rows, lanes, 0, (q + 1) * lanes, 0), 0, 0)
+        if q == 3:
+            keep(gram_of(own_rows, lanes, q, lanes, 0), 0, q)
+            keep(gram_of(own_rows + lanes, lanes, 0, cols, 0), 2, 0)
+        for j in targets(q):
+            stage_copy(q, j).start()
 
     @pl.when(row == 0)
     def _():
         @pl.loop(0, chunks)
         def _(c):
             chain_copy(c).start()
+
+        yh[:, :height] = jnp.zeros((cols, height), BF16)
+        yl[:, :height] = jnp.zeros((cols, height), BF16)
 
     @pl.when(row > 0)
     def _():
@@ -244,88 +293,179 @@
             yh[here, height:] = high
             yl[here, height:] = low
 
-            for q in range(tiles - 1):
-                @pl.when(last & (c == (q + 1) * (chunks // tiles) - 1))
+            for q in range(1, parts - 1):
+                @pl.when(last & (c == (q + 1) * (chunks // parts) - 1))
                 def _():
                     gram_stage(q)
 
-    @pl.when(odd & (row < rows - 1))
-    def _():
-        for q in range(tiles - 1):
-            gram_stage(q)
-
-    @pl.when(odd)
-    def _():
-        gram_stage(tiles - 1)
-
-    def near_copy(side, q):
+    @pl.when(last)
+    def _():
+        gram_stage(parts - 1)
+
+    @pl.when(row < rows - 1)
+    def _():
+        @pl.when(odd)
+        def _():
+            keep(gram_of(half * piece, half * piece, 0, cols, 0), 0, 0)
+
+        @pl.when(parity == 0)
+        def _():
+            keep(gram_of(0, half * piece, 0, cols, 0), 0, 0)
+
+        @pl.when(row >= rows - 3)
+        def _():
+            for j in range(half - 1):
+                @pl.when(2 * j + parity < rows - 3)
+                def _():
+                    pl.semaphore_signal(
+                        go, inc=1, device_id=(sub, 2 * j + parity), device_id_type=MESH
+                    )
+
+        @pl.when(row < rows - 3)
+        def _():
+            pl.semaphore_wait(go, 1)
+
+        for step in range(1, half):
+            gram_copy(step).start()
+
+    at_row = lax.broadcasted_iota(jnp.int32, (cols, cols), 0)
+    at_col = lax.broadcasted_iota(jnp.int32, (cols, cols), 1)
+    place = at_row // piece
+    home = (
+        (at_row % piece) // share * tile
+        + (2 * (place % half) + place // half) * share
+        + at_row % share
+    )
+    perm[...] = jnp.where(home == at_col, 1.0, 0.0).astype(BF16)
+
+    grecv[mine] = gpart[mine]
+
+    def arrival(sem, slot, at):
         return pltpu.make_async_remote_copy(
-            src_ref=gsum.at[stage(q)],
-            dst_ref=nearby.at[side, stage(q)],
-            send_sem=near_send.at[side, q],
-            recv_sem=near_recv.at[side, q],
+            src_ref=gpart.at[0, at],
+            dst_ref=grecv.at[slot, at],
+            send_sem=gram_send.at[0],
+            recv_sem=sem,
+            device_id=(sub, following),
+            device_id_type=MESH,
+        )
+
+    everything = pl.ds(0, parts)
+    for j in range(half):
+        @pl.when((j != mine) & ((j < half - 1) | (parity == 0)))
+        def _():
+            arrival(gram_recv.at[j], j, everything).wait_recv()
+
+    @pl.when(parity == 0)
+    def _():
+        arrival(stage_recv.at[1], half, pl.ds(0, 2)).wait_recv()
+        arrival(stage_recv.at[2], half, pl.ds(2, 1)).wait_recv()
+        arrival(stage_recv.at[3], half, pl.ds(3, 1)).wait_recv()
+
+    @pl.when(odd & (row < rows - 3))
+    def _():
+        arrival(stage_recv.at[2], half - 1, pl.ds(0, 3)).wait_recv()
+        arrival(stage_recv.at[3], half - 1, pl.ds(3, 1)).wait_recv()
+
+    @pl.when(odd & (row == rows - 3))
+    def _():
+        arrival(stage_recv.at[3], half - 1, everything).wait_recv()
+
+    total = []
+    for m in range(parts):
+        value = grecv[0, m]
+        for j in range(1, half):
+            value = value + grecv[j, m]
+        total.append(value + jnp.where(odd, 0.0, grecv[half, m]))
+    total = jnp.concatenate(total, 1)
+    high = total.astype(BF16)
+    rest = total - high.astype(F32)
+    middle, low = split(rest)
+    moved = dot(jnp.concatenate([high, middle, low], 0), perm[...], NN)
+    moved = moved[:piece] + (moved[piece : 2 * piece] + moved[2 * piece :])
+    for k in range(tiles):
+        for l in range(tiles):
+            gsum[k * tiles + l] = moved[k * share : (k + 1) * share, l * tile : (l + 1) * tile]
+
+    def common(owner, other):
+        first = jnp.int32(tiles - 1)
+        second = jnp.int32(0)
+        for k in range(tiles - 1, -1, -1):
+            number = tile_ids[k, owner]
+            hit = number == tile_ids[0, other]
+            for m in range(1, tiles):
+                hit = hit | (number == tile_ids[m, other])
+            first = jnp.where(hit, k, first)
+        for k in range(tiles):
+            number = tile_ids[k, owner]
+            hit = number == tile_ids[0, other]
+            for m in range(1, tiles):
+                hit = hit | (number == tile_ids[m, other])
+            second = jnp.where(hit, k, second)
+        return first, second
+
+    left = jnp.maximum(sub - 1, 0)
+    right = jnp.minimum(sub + 1, subs - 1)
+
+    def near_copy(side):
+        return pltpu.make_async_remote_copy(
+            src_ref=shared.at[side],
+            dst_ref=nearby.at[side],
+            send_sem=near_send.at[side],
+            recv_sem=near_recv.at[side],
             device_id=(sub + 1 if side == 0 else sub - 1, row),
             device_id_type=MESH,
         )
 
-    for q in range(tiles):
-        for j in range(rows // 2):
-            @pl.when(row != 2 * j + 1)
-            def _():
-                pltpu.make_async_remote_copy(
-                    src_ref=gpart.at[0, stage(q)],
-                    dst_ref=grecv.at[j, stage(q)],
-                    send_sem=gram_send.at[q, 0],
-                    recv_sem=gram_recv.at[q, j],
-                    device_id=(sub, following),
-                    device_id_type=MESH,
-                ).wait_recv()
-        total = grecv[0, stage(q)]
-        for j in range(1, rows // 2):
-            total = total + grecv[j, stage(q)]
-        gsum[stage(q)] = total
-
-        @pl.when(has_right)
+    for side, (other, exists) in enumerate(((right, has_right), (left, has_left))):
+        pair = common(sub, other)
+        for p in range(2):
+            for m in range(2):
+                shared[side, 2 * p + m] = gsum[pair[p] * tiles + pair[m]]
+
+        @pl.when(exists)
         def _():
-            near_copy(0, q).start()
-
-        @pl.when(has_left)
-        def _():
-            near_copy(1, q).start()
-
-    for q in range(tiles):
-        @pl.when(has_left)
-        def _():
-            near_copy(0, q).wait_recv()
-
-        @pl.when(has_right)
-        def _():
-            near_copy(1, q).wait_recv()
-
-    def index(k, l):
-        return k * k + l if k >= l else l * l + l + 1 + k
-
-    left = jnp.maximum(sub - 1, 0)
-    right = jnp.minimum(sub + 1, subs - 1)
-    matches = [
-        [
+            near_copy(side).start()
+
+    matches = []
+    for other, exists in ((left, has_left), (right, has_right)):
+        first, second = common(other, sub)
+        matches.append(
             [
-                jnp.where((tile_ids[i, sub] == tile_ids[k, other]) & exists, 1.0, 0.0)
-                for k in range(tiles)
+                [
+                    jnp.where((tile_ids[i, sub] == tile_ids[first, other]) & exists, 1.0, 0.0)
+                    for i in range(tiles)
+                ],
+                [
+                    jnp.where(
+                        (tile_ids[i, sub] == tile_ids[second, other])
+                        & exists
+                        & (first != second),
+                        1.0,
+                        0.0,
+                    )
+                    for i in range(tiles)
+                ],
             ]
-            for i in range(tiles)
-        ]
-        for other, exists in ((left, has_left), (right, has_right))
-    ]
+        )
+
+    @pl.when(has_left)
+    def _():
+        near_copy(0).wait_recv()
+
+    @pl.when(has_right)
+    def _():
+        near_copy(1).wait_recv()
+
     for i in range(tiles):
         across = [
-            [sum(match[i][k] * nearby[side, index(k, m)] for k in range(tiles)) for m in range(tiles)]
+            [match[0][i] * nearby[side, m] + match[1][i] * nearby[side, 2 + m] for m in range(2)]
             for side, match in enumerate(matches)
         ]
         for j in range(tiles):
-            value = gsum[index(i, j)]
+            value = gsum[i * tiles + j]
             for match, taken in zip(matches, across):
-                value = value + sum(match[j][m] * taken[m] for m in range(tiles))
+                value = value + (match[0][j] * taken[0] + match[1][j] * taken[1])
             out[i, :, j * tile : (j + 1) * tile] = value
 
     @pl.when(row < rows - 1)
@@ -334,20 +474,22 @@
         def _(c):
             chain_copy(c).wait_send()
 
-    @pl.when(odd)
-    def _():
-        for q in range(tiles):
-            for step in range(1, rows):
-                gram_copy(q, step).wait_send()
-
-    for q in range(tiles):
-        @pl.when(has_right)
-        def _():
-            near_copy(0, q).wait_send()
-
-        @pl.when(has_left)
-        def _():
-            near_copy(1, q).wait_send()
+        for step in range(1, half):
+            gram_copy(step).wait_send()
+
+    @pl.when(last)
+    def _():
+        for q in range(1, parts):
+            for j in targets(q):
+                stage_copy(q, j).wait_send()
+
+    @pl.when(has_right)
+    def _():
+        near_copy(0).wait_send()
+
+    @pl.when(has_left)
+    def _():
+        near_copy(1).wait_send()
 
 
 def shards(
@@ -357,6 +499,9 @@
     height, cols = coupling.shape[1:]
     tiles, share, _ = interface_block.shape[1:]
     tile = cols // tiles
+    piece = tiles * share
+    lanes = 2 * piece
+    parts = cols // lanes
     locals_ = brows * (brows - 1) // 2
     hbm = pl.BlockSpec(memory_space=pl.ANY)
     vmem = pl.BlockSpec(memory_space=pltpu.VMEM)
@@ -376,17 +521,22 @@
         pltpu.VMEM((height, height), BF16),
         pltpu.VMEM((height, height), BF16),
         pltpu.VMEM((cols, height), F32),
-        pltpu.VMEM((rows, tiles * tiles, share, tile), F32),
-        pltpu.VMEM((rows // 2, tiles * tiles, share, tile), F32),
+        pltpu.VMEM((rows, parts, piece, lanes), F32),
+        pltpu.VMEM((rows // 2 + 1, parts, piece, lanes), F32),
         pltpu.VMEM((tiles * tiles, share, tile), F32),
-        pltpu.VMEM((2, tiles * tiles, share, tile), F32),
+        pltpu.VMEM((cols, cols), BF16),
+        pltpu.VMEM((2, 4, share, tile), F32),
+        pltpu.VMEM((2, 4, share, tile), F32),
         dma((3,)),
         dma((cols // CHUNK,)),
         dma((cols // CHUNK,)),
-        dma((tiles, rows)),
-        dma((tiles, rows // 2)),
-        dma((2, tiles)),
-        dma((2, tiles)),
+        dma((rows // 2,)),
+        dma((rows // 2,)),
+        dma((parts, rows)),
+        dma((parts,)),
+        dma((2,)),
+        dma((2,)),
+        pltpu.SemaphoreType.REGULAR,
     ]
     contribution = pl.pallas_call(
         functools.partial(kernel, subs, rows),

time: 107 us -> 102 us (0.953)
  Pallas kernels: 105 us -> 99.6 us
    pallas_call x1, Pallas kernels: 105 us -> 99.6 us  [shards(): pl.pallas_call(functools.partial(kernel, subs, rows), out_shape=jax.Shape...]
where the time goes in v3:
time: 102 us; the launch traced here: 101 us
  Pallas kernels  99.6 us (98%)
  other arithmetic  1.58 us (2%)
    pallas_call x1, Pallas kernels, shards(): pl.pallas_call(functools.partial(kernel, subs, rows), out_shape=jax.Shape...  99.6 us

profile of v3, /device:TPU:107, one launch (start us, length us, event | category | flops | bytes accessed | tf_op | source)
XLA Modules:
  0.0 101.2 jit_solution(1080195993435120529)
XLA Ops:
  0.0 0.0 copy-start
  0.0 99.6 %shard_map.64 = f32[4,16,512]{2,1,0:T(8,128)} custom-call(f32[4,3,256,256]{3,2,1,0:T(8,128)} %bitcast.7, f32[4,256,256]{2,1,0:T(8,128)} %bitcast.9, s32[3,1,4]{2,1,0:T(1,128)} %bitcast.11, f32[1024,512]{1,0:T(8,128)} %bitcast.8, s32[4,32]{1,0:T(4,128)} %bitcast.10), custom_call_target="tpu_custom_call" | custom-call | tf_op jit(solution)/shard_map/pallas_call | solution.py:541
  99.6 0.0 copy-done
  99.6 1.6 %bitcast_subtract_fusion = f32[1,4,16,512]{3,2,1,0:T(8,128)} fusion(f32[1,4,16,512]{3,2,1,0:T(8,128)S(1)} %copy-done, f32[4,16,512]{2,1,0:T(8,128)} %shard_map.64), kind=kLoop, calls=%fused_computation | loop fusion | flops 32768 | bytes 393216 | tf_op jit(solution)/shard_map/sub | solution.py:557
Async XLA Ops:
  0.0 99.6 %copy-start = (f32[1,4,16,512]{3,2,1,0:T(8,128)S(1)}, f32[1,4,16,512]{3,2,1,0:T(8,128)}, u32[]{:S(2)}) copy-start(f32[1,4,16,512]{3,2,1,0:T(8,128)} %param.10) | copy-start | bytes 393220

commit v4 on v3

--- a/solution.py
+++ b/solution.py
@@ -54,6 +54,7 @@
     gpart,
     grecv,
     gsum,
+    gsum_early,
     perm,
     shared,
     nearby,
@@ -88,7 +89,7 @@
     loads = [
         pltpu.make_async_copy(source, target, load_sem.at[i])
         for i, (source, target) in enumerate(
-            ((inverse_hbm, inverse), (factor_hbm, factor), (coupling_hbm, coupling))
+            ((inverse_hbm, inverse), (coupling_hbm, coupling), (factor_hbm, factor))
         )
     ]
     for load in loads:
@@ -134,6 +135,14 @@
         ih[r] = high
         il[r] = low
     loads[1].wait()
+    order = [
+        k * tile + (2 * j + p) * share for p in range(2) for j in range(half) for k in range(tiles)
+    ]
+    for r in range(brows):
+        natural = coupling[span(r), :].T
+        high, low = split(jnp.concatenate([natural[n : n + share] for n in order], 0))
+        yt[:, span(r)] = dot3(high, low, ih[r], il[r])
+    loads[2].wait()
     for r in range(1, brows):
         for offset in range(1, r + 1):
             high, low = split(at_offset(r, offset))
@@ -141,19 +150,14 @@
             nh[local(r, offset)] = high
             nl[local(r, offset)] = low
 
-    loads[2].wait()
     for r in range(brows):
-        natural = coupling[span(r), :].T
-        order = [
-            k * tile + (2 * j + p) * share for p in range(2) for j in range(half) for k in range(tiles)
-        ]
-        high, low = split(jnp.concatenate([natural[n : n + share] for n in order], 0))
-        solved = dot3(high, low, ih[r], il[r])
+        solved = yt[:, span(r)]
         for offset in range(r, 0, -1):
             s = own(r - offset)
             n = local(r, offset)
             solved = solved - dot3(yh[:, s], yl[:, s], nh[n], nl[n])
-        yt[:, span(r)] = solved
+        if r > 0:
+            yt[:, span(r)] = solved
         high, low = split(solved)
         yh[:, own(r)] = high
         yl[:, own(r)] = low
@@ -218,24 +222,32 @@
             device_id_type=MESH,
         )
 
+    far_first = sorted(range(0, rows, 2), key=lambda j: -min(half - 1 - j // 2, j // 2 + 1))
+
     def targets(q):
-        evens = [] if q == 0 else list(range(0, rows, 2))
         odds = [j for j in range(1, rows - 1, 2) if (half + j // 2) // 2 <= q]
-        return odds + evens
+        return (far_first if q > 0 else []), odds
+
+    def send_stage(q, pieces):
+        for j in pieces:
+            stage_copy(q, j).start()
 
     def gram_stage(q):
         own_rows = half * piece
+        evens, odds = targets(q)
         if q == 1:
             keep(gram_of(0, own_rows, 0, 2 * lanes, height), half, 0)
-        if q >= 2:
+        else:
             keep(gram_of(0, own_rows, q, lanes, height), half, q)
+        send_stage(q, evens)
         if q == 2:
             keep(gram_of(own_rows, lanes, 0, (q + 1) * lanes, 0), 0, 0)
+            send_stage(q, odds)
         if q == 3:
+            keep(gram_of(own_rows + lanes, lanes, 0, cols, 0), 2, 0)
+            send_stage(q, odds[-1:])
             keep(gram_of(own_rows, lanes, q, lanes, 0), 0, q)
-            keep(gram_of(own_rows + lanes, lanes, 0, cols, 0), 2, 0)
-        for j in targets(q):
-            stage_copy(q, j).start()
+            send_stage(q, odds[:-1])
 
     @pl.when(row == 0)
     def _():
@@ -302,90 +314,45 @@
     def _():
         gram_stage(parts - 1)
 
-    @pl.when(row < rows - 1)
-    def _():
-        @pl.when(odd)
+    def release(source, to):
+        @pl.when(row == source)
         def _():
-            keep(gram_of(half * piece, half * piece, 0, cols, 0), 0, 0)
-
-        @pl.when(parity == 0)
+            pl.semaphore_signal(go, inc=1, device_id=(sub, to), device_id_type=MESH)
+
+    release(rows - 2, rows - 4)
+    for to in range(rows - 4):
+        release(rows - 3 if to % 2 else rows - 4, to)
+
+    def send_gram(source, steps):
+        @pl.when(row == source)
         def _():
-            keep(gram_of(0, half * piece, 0, cols, 0), 0, 0)
-
-        @pl.when(row >= rows - 3)
-        def _():
-            for j in range(half - 1):
-                @pl.when(2 * j + parity < rows - 3)
-                def _():
-                    pl.semaphore_signal(
-                        go, inc=1, device_id=(sub, 2 * j + parity), device_id_type=MESH
-                    )
-
-        @pl.when(row < rows - 3)
-        def _():
-            pl.semaphore_wait(go, 1)
-
+            for step in steps:
+                gram_copy(step).start()
+
+    def gram_half(h):
+        for p in range(2):
+            @pl.when((parity == p) & (row < rows - 1))
+            def _():
+                keep(gram_of(p * half * piece + h * lanes, lanes, 0, cols, 0), 2 * h, 0)
+
+    gram_half(0)
+    send_gram(rows - 2, (2, 1))
+    send_gram(rows - 3, (2, 3))
+    send_gram(rows - 4, (3,))
+    gram_half(1)
+    send_gram(rows - 2, (3,))
+    send_gram(rows - 3, (1,))
+
+    @pl.when(row < rows - 3)
+    def _():
+        pl.semaphore_wait(go, 1)
+
+    send_gram(rows - 4, (2, 1))
+
+    @pl.when(row < rows - 4)
+    def _():
         for step in range(1, half):
             gram_copy(step).start()
-
-    at_row = lax.broadcasted_iota(jnp.int32, (cols, cols), 0)
-    at_col = lax.broadcasted_iota(jnp.int32, (cols, cols), 1)
-    place = at_row // piece
-    home = (
-        (at_row % piece) // share * tile
-        + (2 * (place % half) + place // half) * share
-        + at_row % share
-    )
-    perm[...] = jnp.where(home == at_col, 1.0, 0.0).astype(BF16)
-
-    grecv[mine] = gpart[mine]
-
-    def arrival(sem, slot, at):
-        return pltpu.make_async_remote_copy(
-            src_ref=gpart.at[0, at],
-            dst_ref=grecv.at[slot, at],
-            send_sem=gram_send.at[0],
-            recv_sem=sem,
-            device_id=(sub, following),
-            device_id_type=MESH,
-        )
-
-    everything = pl.ds(0, parts)
-    for j in range(half):
-        @pl.when((j != mine) & ((j < half - 1) | (parity == 0)))
-        def _():
-            arrival(gram_recv.at[j], j, everything).wait_recv()
-
-    @pl.when(parity == 0)
-    def _():
-        arrival(stage_recv.at[1], half, pl.ds(0, 2)).wait_recv()
-        arrival(stage_recv.at[2], half, pl.ds(2, 1)).wait_recv()
-        arrival(stage_recv.at[3], half, pl.ds(3, 1)).wait_recv()
-
-    @pl.when(odd & (row < rows - 3))
-    def _():
-        arrival(stage_recv.at[2], half - 1, pl.ds(0, 3)).wait_recv()
-        arrival(stage_recv.at[3], half - 1, pl.ds(3, 1)).wait_recv()
-
-    @pl.when(odd & (row == rows - 3))
-    def _():
-        arrival(stage_recv.at[3], half - 1, everything).wait_recv()
-
-    total = []
-    for m in range(parts):
-        value = grecv[0, m]
-        for j in range(1, half):
-            value = value + grecv[j, m]
-        total.append(value + jnp.where(odd, 0.0, grecv[half, m]))
-    total = jnp.concatenate(total, 1)
-    high = total.astype(BF16)
-    rest = total - high.astype(F32)
-    middle, low = split(rest)
-    moved = dot(jnp.concatenate([high, middle, low], 0), perm[...], NN)
-    moved = moved[:piece] + (moved[piece : 2 * piece] + moved[2 * piece :])
-    for k in range(tiles):
-        for l in range(tiles):
-            gsum[k * tiles + l] = moved[k * share : (k + 1) * share, l * tile : (l + 1) * tile]
 
     def common(owner, other):
         first = jnp.int32(tiles - 1)
@@ -407,26 +374,7 @@
     left = jnp.maximum(sub - 1, 0)
     right = jnp.minimum(sub + 1, subs - 1)
 
-    def near_copy(side):
-        return pltpu.make_async_remote_copy(
-            src_ref=shared.at[side],
-            dst_ref=nearby.at[side],
-            send_sem=near_send.at[side],
-            recv_sem=near_recv.at[side],
-            device_id=(sub + 1 if side == 0 else sub - 1, row),
-            device_id_type=MESH,
-        )
-
-    for side, (other, exists) in enumerate(((right, has_right), (left, has_left))):
-        pair = common(sub, other)
-        for p in range(2):
-            for m in range(2):
-                shared[side, 2 * p + m] = gsum[pair[p] * tiles + pair[m]]
-
-        @pl.when(exists)
-        def _():
-            near_copy(side).start()
-
+    pairs = [common(sub, right), common(sub, left)]
     matches = []
     for other, exists in ((left, has_left), (right, has_right)):
         first, second = common(other, sub)
@@ -449,6 +397,98 @@
             ]
         )
 
+    at_row = lax.broadcasted_iota(jnp.int32, (cols, cols), 0)
+    at_col = lax.broadcasted_iota(jnp.int32, (cols, cols), 1)
+    place = at_row // piece
+    home = (
+        (at_row % piece) // share * tile
+        + (2 * (place % half) + place // half) * share
+        + at_row % share
+    )
+    perm[...] = jnp.where(home == at_col, 1.0, 0.0).astype(BF16)
+
+    grecv[mine] = gpart[mine]
+
+    def arrival(sem, slot, at):
+        return pltpu.make_async_remote_copy(
+            src_ref=gpart.at[0, at],
+            dst_ref=grecv.at[slot, at],
+            send_sem=gram_send.at[0],
+            recv_sem=sem,
+            device_id=(sub, following),
+            device_id_type=MESH,
+        )
+
+    for j in range(half):
+        @pl.when((j != mine) & ((j < half - 1) | (parity == 0)))
+        def _():
+            arrival(gram_recv.at[j], j, pl.ds(0, parts)).wait_recv()
+
+    @pl.when(parity == 0)
+    def _():
+        arrival(stage_recv.at[1], half, pl.ds(0, 2)).wait_recv()
+        arrival(stage_recv.at[2], half, pl.ds(2, 1)).wait_recv()
+
+    @pl.when(odd & (row < rows - 3))
+    def _():
+        arrival(stage_recv.at[2], half - 1, pl.ds(0, 3)).wait_recv()
+
+    @pl.when(odd & (row == rows - 3))
+    def _():
+        arrival(stage_recv.at[3], half - 1, pl.ds(0, parts)).wait_recv()
+
+    def placed(blocks, start):
+        value = jnp.concatenate(blocks, 1)
+        high = value.astype(BF16)
+        middle, low = split(value - high.astype(F32))
+        moved = dot(
+            jnp.concatenate([high, middle, low], 0),
+            perm[start * lanes : (start + len(blocks)) * lanes, :],
+            NN,
+        )
+        return moved[:piece] + (moved[piece : 2 * piece] + moved[2 * piece :])
+
+    def summed(m):
+        value = grecv[0, m]
+        for j in range(1, half):
+            value = value + grecv[j, m]
+        return value + jnp.where(odd, 0.0, grecv[half, m])
+
+    gsum_early[...] = placed([summed(m) for m in range(parts - 1)], 0)
+
+    @pl.when(parity == 0)
+    def _():
+        arrival(stage_recv.at[3], half, pl.ds(3, 1)).wait_recv()
+
+    @pl.when(odd & (row < rows - 3))
+    def _():
+        arrival(stage_recv.at[3], half - 1, pl.ds(3, 1)).wait_recv()
+
+    moved = gsum_early[...] + placed([summed(parts - 1)], parts - 1)
+    for k in range(tiles):
+        for l in range(tiles):
+            gsum[k * tiles + l] = moved[k * share : (k + 1) * share, l * tile : (l + 1) * tile]
+
+    def near_copy(side):
+        return pltpu.make_async_remote_copy(
+            src_ref=shared.at[side],
+            dst_ref=nearby.at[side],
+            send_sem=near_send.at[side],
+            recv_sem=near_recv.at[side],
+            device_id=(sub + 1 if side == 0 else sub - 1, row),
+            device_id_type=MESH,
+        )
+
+    for side, (other, exists) in enumerate(((right, has_right), (left, has_left))):
+        pair = pairs[side]
+        for p in range(2):
+            for m in range(2):
+                shared[side, 2 * p + m] = gsum[pair[p] * tiles + pair[m]]
+
+        @pl.when(exists)
+        def _():
+            near_copy(side).start()
+
     @pl.when(has_left)
     def _():
         near_copy(0).wait_recv()
@@ -480,7 +520,7 @@
     @pl.when(last)
     def _():
         for q in range(1, parts):
-            for j in targets(q):
+            for j in sum(targets(q), []):
                 stage_copy(q, j).wait_send()
 
     @pl.when(has_right)
@@ -524,6 +564,7 @@
         pltpu.VMEM((rows, parts, piece, lanes), F32),
         pltpu.VMEM((rows // 2 + 1, parts, piece, lanes), F32),
         pltpu.VMEM((tiles * tiles, share, tile), F32),
+        pltpu.VMEM((piece, cols), F32),
         pltpu.VMEM((cols, cols), BF16),
         pltpu.VMEM((2, 4, share, tile), F32),
         pltpu.VMEM((2, 4, share, tile), F32),

time: 102 us -> 101 us (level)
  Pallas kernels: 99.6 us -> 97.8 us
    pallas_call x1, Pallas kernels: 99.6 us -> 97.8 us  [shards(): pl.pallas_call(functools.partial(kernel, subs, rows), out_shape=jax.Shape...]
where the time goes in v4:
time: 101 us; the launch traced here: 99.4 us
  Pallas kernels  97.8 us (97%)
  other arithmetic  1.58 us (2%)
    pallas_call x1, Pallas kernels, shards(): pl.pallas_call(functools.partial(kernel, subs, rows), out_shape=jax.Shape...  97.8 us

profile of v4, /device:TPU:107, one launch (start us, length us, event | category | flops | bytes accessed | tf_op | source)
XLA Modules:
  0.0 99.4 jit_solution(1460213095367083272)
XLA Ops:
  0.0 0.0 copy-start
  0.0 97.8 %shard_map.64 = f32[4,16,512]{2,1,0:T(8,128)} custom-call(f32[4,3,256,256]{3,2,1,0:T(8,128)} %bitcast.7, f32[4,256,256]{2,1,0:T(8,128)} %bitcast.9, s32[3,1,4]{2,1,0:T(1,128)} %bitcast.11, f32[1024,512]{1,0:T(8,128)} %bitcast.8, s32[4,32]{1,0:T(4,128)} %bitcast.10), custom_call_target="tpu_custom_call" | custom-call | tf_op jit(solution)/shard_map/pallas_call | solution.py:582
  97.8 0.0 copy-done
  97.8 1.6 %bitcast_subtract_fusion = f32[1,4,16,512]{3,2,1,0:T(8,128)} fusion(f32[1,4,16,512]{3,2,1,0:T(8,128)S(1)} %copy-done, f32[4,16,512]{2,1,0:T(8,128)} %shard_map.64), kind=kLoop, calls=%fused_computation | loop fusion | flops 32768 | bytes 393216 | tf_op jit(solution)/shard_map/sub | solution.py:598
Async XLA Ops:
  0.0 97.8 %copy-start = (f32[1,4,16,512]{3,2,1,0:T(8,128)S(1)}, f32[1,4,16,512]{3,2,1,0:T(8,128)}, u32[]{:S(2)}) copy-start(f32[1,4,16,512]{3,2,1,0:T(8,128)} %param.10) | copy-start | bytes 393220

commit v5 on v4

--- a/solution.py
+++ b/solution.py
@@ -586,7 +586,7 @@
         out_specs=vmem,
         scratch_shapes=scratch,
         compiler_params=pltpu.CompilerParams(
-            collective_id=0, has_side_effects=True, vmem_limit_bytes=60 * 1024 * 1024
+            collective_id=0, has_side_effects=True, vmem_limit_bytes=53 * 1024 * 1024
         ),
     )(
         factor_blocks[0],

time: 101 us -> 101 us (level)
  local copies, waits for them, and re-layouts: 0.01 us -> 1.36 us
    unnamed x2 -> x6, local copies, waits for them, and re-layouts: 0.01 us -> 1.36 us
where the time goes in v5:
time: 101 us; the launch traced here: 98.9 us
  Pallas kernels  96.8 us (96%)
  local copies, waits for them, and re-layouts  1.36 us (1%)
    pallas_call x1, Pallas kernels, shards(): pl.pallas_call(functools.partial(kernel, subs, rows), out_shape=jax.Shape...  96.8 us

profile of v5, /device:TPU:107, one launch (start us, length us, event | category | flops | bytes accessed | tf_op | source)
XLA Modules:
  0.0 98.9 jit_solution(2278236682851979564)
XLA Ops:
  0.0 0.0 copy-start
  0.0 0.7 copy-done
  0.7 0.0 copy-start.1
  0.7 0.7 copy-done.1
  1.4 0.0 copy-start.2
  1.4 96.8 %shard_map.64 = f32[4,16,512]{2,1,0:T(8,128)S(1)} custom-call(f32[4,3,256,256]{3,2,1,0:T(8,128)} %bitcast.9, f32[4,256,256]{2,1,0:T(8,128)} %bitcast.11, s32[3,1,4]{2,1,0:T(1,128)S(1)} %bitcast.8, f32[1024,512]{1,0:T(8,128)} %bitcast.10, s32[4,32]{1,0:T(4,128)S(1)} %bitcast.7), custom_call_target="tpu_custom_call" | custom-call | tf_op jit(solution)/shard_map/pallas_call | solution.py:582
  98.2 0.0 copy-done.2
  98.2 0.7 bitcast_subtract_fusion
Async XLA Ops:
  0.0 0.7 copy-start
  0.7 0.7 copy-start.1
  1.4 96.9 %copy-start.2 = (f32[1,4,16,512]{3,2,1,0:T(8,128)S(1)}, f32[1,4,16,512]{3,2,1,0:T(8,128)}, u32[]{:S(2)}) copy-start(f32[1,4,16,512]{3,2,1,0:T(8,128)} %param.10) | copy-start | bytes 393220
